TPU v7x, 512 devices: a whole 4x8x8 slice. The times are simulated.
512 devices in a mesh: grp: 2 (over y_lo), zt: 16 (over x, y_hi), xy: 16 (over z, core).
Axes of the slice: x: 4, y: 8 (y_hi: 4, y_lo: 2; y = y_hi * 2 + y_lo), z: 8, core: 2. Of those that a mesh axis runs over, the one named last changes fastest.
Arguments:
- source: float32 [2, 2, 3, 32, 64, 128], P('grp', None, None, 'xy', 'zt'), may hold values from -6 to 6
- links: float32 [4, 2, 3, 3, 32, 64, 128], P('grp', None, None, None, 'xy', 'zt'), may hold values from -2 to 2
- shifts: float32 [12], replicated, may hold values from 0.01 to 0.5
- residues: float32 [12], replicated, may hold values from 0.05 to 0.5
- mass: float32 [1], replicated, may hold values from 0.1 to 0.5
Outputs:
- rational: float32 [2, 2, 3, 32, 64, 128], P('grp', None, None, 'xy', 'zt')
- action: float32 [1], replicated
All inputs are finite; a program needn't handle non-finite values.
Results may differ from a plain program's by a relative error of at most 0.0003.
Values sent between devices are 32-bit elements; how exact they have to be, the bound alone decides.
No kernel may reach another device: no remote copies, remote signals or barrier semaphores. Data moves between devices by JAX's collectives and lax.ppermute only.
A program may use at most 64 MiB of HBM per device.

v0:
```python
import jax
import jax.numpy as jnp
from jax import lax
from jax.sharding import Mesh
from jax.sharding import PartitionSpec as P

NY = 2
NZ = 64
ITERS = 8
XY = ("xy_0", "xy_1")
ZT = ("zt_0", "zt_1")
ZT_XY = ("zt_0", "zt_1", "xy_0", "xy_1")
GRP_ZT_XY = ("grp", "zt_0", "zt_1", "xy_0", "xy_1")


def copy_for_each(x, axis):
    peers = lax.axis_size(axis)
    return lax.all_to_all(jnp.broadcast_to(x[None], (peers, *x.shape)), axis, 0, 0, tiled=True)


def laid_out(parts, dim):
    dims = list(parts.shape[1:])
    dims[dim] *= parts.shape[0]
    return jnp.moveaxis(parts, 0, dim).reshape(dims)


def gathered_copies(x, axis, dim):
    parts = copy_for_each(x, axis)
    return laid_out(parts, dim)


def shifted(block, axis, distance):
    devices = range(lax.axis_size(axis))
    route = [((i - distance) % len(devices), i) for i in devices]
    return lax.ppermute(block, axis, route)


def extended(x, sides, width):
    edges = {}
    for axis, dim in sides:
        peers, length = (lax.axis_size(axis), x.shape[dim])
        up = [(i, (i + 1) % peers) for i in range(peers)]
        last = lax.slice_in_dim(x, length - width, length, axis=dim)
        initial = lax.slice_in_dim(x, 0, width, axis=dim)
        edges[dim] = (
            lax.ppermute(last, axis, up),
            lax.ppermute(initial, axis, [(b, a) for a, b in up]),
        )
    done = []
    for _, dim in sides:
        low, high = edges[dim]
        around = [(width, width) if d in done else (0, 0) for d in range(x.ndim)]
        x = jnp.concatenate([jnp.pad(low, around), x, jnp.pad(high, around)], axis=dim)
        done.append(dim)
    return x


def one_axis_at_a_time(x, axes):
    for axis in axes:
        x = lax.psum(x, axis)
    return x


def sign_of(values):
    return (1 - 2 * (values % 2)).astype(jnp.float32)


def phases(coord_x, coord_t, last_t):
    yz_index = jnp.arange(NY * NZ, dtype=jnp.int32)
    ycoord = yz_index // NZ
    zcoord = yz_index % NZ
    unity = jnp.ones((coord_x.shape[0], coord_t.shape[0], NY * NZ), jnp.float32)
    boundary = jnp.where(coord_t == last_t, -1.0, 1.0).astype(jnp.float32)
    eta_y = sign_of(coord_x)[:, None, None] * unity
    eta_z = sign_of(coord_x[:, None, None] + ycoord[None, None, :]) * unity
    eta_t = (
        sign_of(coord_x[:, None, None] + ycoord[None, None, :] + zcoord[None, None, :])
        * boundary[None, :, None]
    )
    return jnp.stack([unity, eta_y, eta_z, eta_t])


def times_link(link, field):
    real = jnp.sum(
        link[0][None] * field[:, 0][:, None] - link[1][None] * field[:, 1][:, None], axis=2
    )
    imag = jnp.sum(
        link[0][None] * field[:, 1][:, None] + link[1][None] * field[:, 0][:, None], axis=2
    )
    return jnp.stack([real, imag], axis=1)


def times_adjoint(link, field):
    real = jnp.sum(
        link[0][None] * field[:, 0][:, :, None] + link[1][None] * field[:, 1][:, :, None], axis=1
    )
    imag = jnp.sum(
        link[0][None] * field[:, 1][:, :, None] - link[1][None] * field[:, 0][:, :, None], axis=1
    )
    return jnp.stack([real, imag], axis=1)


def roll_ycoord(values, offset):
    return jnp.roll(values, offset * NZ, axis=-1)


def roll_zcoord(values, offset):
    shape = values.shape
    return jnp.roll(values.reshape(shape[:-1] + (NY, NZ)), offset, axis=-1).reshape(shape)


def hopping(field, link):
    inner_field = field[..., 1:-1, 1:-1, :]
    inner_link = link[..., 1:-1, 1:-1, :]
    total = times_link(inner_link[0], field[..., 2:, 1:-1, :]) - times_adjoint(
        link[0][..., :-2, 1:-1, :], field[..., :-2, 1:-1, :]
    )
    total = (
        total
        + times_link(inner_link[1], roll_ycoord(inner_field, -1))
        - roll_ycoord(times_adjoint(inner_link[1], inner_field), 1)
    )
    total = (
        total
        + times_link(inner_link[2], roll_zcoord(inner_field, -1))
        - roll_zcoord(times_adjoint(inner_link[2], inner_field), 1)
    )
    total = (
        total
        + times_link(inner_link[3], field[..., 1:-1, 2:, :])
        - times_adjoint(link[3][..., 1:-1, :-2, :], field[..., 1:-1, :-2, :])
    )
    return 0.5 * total


def local_dot(left, right):
    return jnp.sum(left * right, axis=(1, 2, 3, 4, 5))


def spread(values):
    return values.reshape(values.shape + (1, 1, 1, 1, 1))


def on_device(source, links, shifts, residues, mass):
    all_links = gathered_copies(links, "grp", 0)
    cells_x = source.shape[3]
    cells_t = source.shape[4]
    coord_x = lax.axis_index(XY) * cells_x + jnp.arange(cells_x, dtype=jnp.int32)
    coord_t = lax.axis_index(ZT) * cells_t + jnp.arange(cells_t, dtype=jnp.int32)
    eta = phases(coord_x, coord_t, cells_t * lax.axis_size(ZT) - 1)
    folded = all_links * eta[:, None, None, None]
    mass_sq = mass[0] * mass[0]
    rim_x = shifted(folded[0][:, :, :, -1:, :, :], XY, 1)
    rim_t = shifted(folded[3][:, :, :, :, -1:, :], ZT, 1)
    wide_links = jnp.pad(folded, ((0, 0), (0, 0), (0, 0), (0, 0), (1, 1), (1, 1), (0, 0)))
    wide_links = wide_links.at[0, :, :, :, 0:1, 1:-1, :].set(rim_x)
    wide_links = wide_links.at[3, :, :, :, 1:-1, 0:1, :].set(rim_t)

    def with_faces(field):
        return extended(field, ((ZT, 4), (XY, 3)), 1)

    shift_col = shifts[:, None]
    members = source.shape[0]
    residual = source
    direction = source
    solutions = jnp.zeros((shifts.shape[0],) + source.shape, jnp.float32)
    directions = jnp.broadcast_to(source[None], solutions.shape)
    norm_now = one_axis_at_a_time(local_dot(source, source), ZT_XY)
    zeta_now = jnp.ones((shifts.shape[0], members), jnp.float32)
    zeta_old = jnp.ones((shifts.shape[0], members), jnp.float32)
    alpha_old = jnp.ones((members,), jnp.float32)
    beta_old = jnp.zeros((members,), jnp.float32)
    for iteration in range(ITERS):
        first_hop = hopping(with_faces(direction), wide_links)
        image = mass_sq * direction - hopping(with_faces(first_hop), wide_links)
        curvature_sum, cross_sum, image_sum = (
            one_axis_at_a_time(local_dot(direction, image), ZT_XY),
            one_axis_at_a_time(local_dot(residual, image), ZT_XY),
            one_axis_at_a_time(local_dot(image, image), ZT_XY),
        )
        alpha_now = norm_now / curvature_sum
        zeta_new = (
            zeta_now
            * zeta_old
            * alpha_old
            / (
                alpha_now * beta_old * (zeta_old - zeta_now)
                + zeta_old * alpha_old * (1.0 + shift_col * alpha_now)
            )
        )
        alpha_shift = alpha_now * zeta_new / zeta_now
        solutions = solutions + spread(alpha_shift) * directions
        if iteration + 1 < ITERS:
            residual = residual - spread(alpha_now) * image
            norm_next = norm_now - 2.0 * alpha_now * cross_sum + alpha_now * alpha_now * image_sum
            beta_now = norm_next / norm_now
            beta_shift = beta_now * (zeta_new / zeta_now) ** 2
            direction = residual + spread(beta_now) * direction
            directions = spread(zeta_new) * residual[None] + spread(beta_shift) * directions
            zeta_old = zeta_now
            zeta_now = zeta_new
            alpha_old = alpha_now
            beta_old = beta_now
            norm_now = norm_next
    rational = jnp.sum(residues.reshape((-1, 1, 1, 1, 1, 1, 1)) * solutions, axis=0)
    total = one_axis_at_a_time(jnp.sum(source * rational), GRP_ZT_XY)
    site_count = (
        members
        * lax.axis_size("grp")
        * cells_x
        * lax.axis_size(XY)
        * cells_t
        * lax.axis_size(ZT)
        * NY
        * NZ
    )
    action = (total / site_count).reshape(1)
    return (rational, action)


def solution(mesh):
    torus = Mesh(
        mesh.devices.reshape(mesh.shape["grp"], 4, 4, 8, 2), ("grp", "zt_0", "zt_1", "xy_0", "xy_1")
    )
    placed = (
        P("grp", None, None, XY, ZT, None),
        P("grp", None, None, None, XY, ZT, None),
        P(),
        P(),
        P(),
    )
    return jax.shard_map(
        on_device,
        mesh=torus,
        in_specs=placed,
        out_specs=(P("grp", None, None, XY, ZT, None), P()),
        check_vma=False,
    )
```

profile of v0, /device:TPU:27, one launch (start us, length us, event | category | flops | bytes accessed | tf_op | source)
XLA Modules:
  0.0 693.6 jit_solution(17741882495285166193)
XLA Ops:
  60.1 10.3 %all-reduce.46 = (f32[1]{0:T(128)}, f32[1]{0:T(128)}, f32[1]{0:T(128)}) all-reduce(f32[1]{0:T(128)} %get-tuple-element.455, f32[1]{0:T(128)} %get-tuple-element.456, f32[1]{0:T(128)} %get-tuple-element.457), channel_id=1, replica_groups=mesh['grp'=2,'zt_0'=4,'zt_1'=4,'xy_0'=8,'xy_1'=2] {'zt_1'}, use_global_device_ids=true, to_apply=%region_2.3 | all-reduce | flops 3 | bytes 24 | tf_op jit(solution)/shard_map/psum | solution.py:60
  70.4 16.2 %all-reduce.39 = (f32[1]{0:T(128)}, f32[1]{0:T(128)}, f32[1]{0:T(128)}) all-reduce(f32[1]{0:T(128)} %get-tuple-element.434, f32[1]{0:T(128)} %get-tuple-element.435, f32[1]{0:T(128)} %get-tuple-element.436), channel_id=1, replica_groups=mesh['grp'=2,'zt_0'=4,'zt_1'=4,'xy_0'=8,'xy_1'=2] {'xy_0'}, use_global_device_ids=true, to_apply=%region_3.4 | all-reduce | flops 3 | bytes 24 | tf_op jit(solution)/shard_map/psum | solution.py:60
  86.6 8.8 %all-reduce.60 = (f32[1]{0:T(128)}, f32[1]{0:T(128)}, f32[1]{0:T(128)}) all-reduce(f32[1]{0:T(128)} %get-tuple-element.413, f32[1]{0:T(128)} %get-tuple-element.414, f32[1]{0:T(128)} %get-tuple-element.415), channel_id=1, replica_groups=mesh['grp'=2,'zt_0'=4,'zt_1'=4,'xy_0'=8,'xy_1'=2] {'xy_1'}, use_global_device_ids=true, to_apply=%region_4.5 | all-reduce | flops 3 | bytes 24 | tf_op jit(solution)/shard_map/psum | solution.py:60
  131.4 9.3 %all-reduce.52 = (f32[1]{0:T(128)}, f32[1]{0:T(128)}, f32[1]{0:T(128)}) all-reduce(f32[1]{0:T(128)} %bitcast.139, f32[1]{0:T(128)} %bitcast.143, f32[1]{0:T(128)} %bitcast.144), channel_id=1, replica_groups=mesh['grp'=2,'zt_0'=4,'zt_1'=4,'xy_0'=8,'xy_1'=2] {'zt_0'}, use_global_device_ids=true, to_apply=%region_80.81 | all-reduce | flops 3 | bytes 24 | tf_op jit(solution)/shard_map/psum | solution.py:60
  140.7 10.2 %all-reduce.45 = (f32[1]{0:T(128)}, f32[1]{0:T(128)}, f32[1]{0:T(128)}) all-reduce(f32[1]{0:T(128)} %get-tuple-element.452, f32[1]{0:T(128)} %get-tuple-element.453, f32[1]{0:T(128)} %get-tuple-element.454), channel_id=1, replica_groups=mesh['grp'=2,'zt_0'=4,'zt_1'=4,'xy_0'=8,'xy_1'=2] {'zt_1'}, use_global_device_ids=true, to_apply=%region_81.82 | all-reduce | flops 3 | bytes 24 | tf_op jit(solution)/shard_map/psum | solution.py:60
  150.9 14.6 %all-reduce.38 = (f32[1]{0:T(128)}, f32[1]{0:T(128)}, f32[1]{0:T(128)}) all-reduce(f32[1]{0:T(128)} %get-tuple-element.431, f32[1]{0:T(128)} %get-tuple-element.432, f32[1]{0:T(128)} %get-tuple-element.433), channel_id=1, replica_groups=mesh['grp'=2,'zt_0'=4,'zt_1'=4,'xy_0'=8,'xy_1'=2] {'xy_0'}, use_global_device_ids=true, to_apply=%region_82.83 | all-reduce | flops 3 | bytes 24 | tf_op jit(solution)/shard_map/psum | solution.py:60
  165.5 8.9 %all-reduce.59 = (f32[1]{0:T(128)}, f32[1]{0:T(128)}, f32[1]{0:T(128)}) all-reduce(f32[1]{0:T(128)} %get-tuple-element.410, f32[1]{0:T(128)} %get-tuple-element.411, f32[1]{0:T(128)} %get-tuple-element.412), channel_id=1, replica_groups=mesh['grp'=2,'zt_0'=4,'zt_1'=4,'xy_0'=8,'xy_1'=2] {'xy_1'}, use_global_device_ids=true, to_apply=%region_83.84 | all-reduce | flops 3 | bytes 24 | tf_op jit(solution)/shard_map/psum | solution.py:60
  208.8 9.1 %all-reduce.51 = (f32[1]{0:T(128)}, f32[1]{0:T(128)}, f32[1]{0:T(128)}) all-reduce(f32[1]{0:T(128)} %bitcast.204, f32[1]{0:T(128)} %bitcast.208, f32[1]{0:T(128)} %bitcast.209), channel_id=1, replica_groups=mesh['grp'=2,'zt_0'=4,'zt_1'=4,'xy_0'=8,'xy_1'=2] {'zt_0'}, use_global_device_ids=true, to_apply=%region_127.128 | all-reduce | flops 3 | bytes 24 | tf_op jit(solution)/shard_map/psum | solution.py:60
  217.9 10.6 %all-reduce.44 = (f32[1]{0:T(128)}, f32[1]{0:T(128)}, f32[1]{0:T(128)}) all-reduce(f32[1]{0:T(128)} %get-tuple-element.449, f32[1]{0:T(128)} %get-tuple-element.450, f32[1]{0:T(128)} %get-tuple-element.451), channel_id=1, replica_groups=mesh['grp'=2,'zt_0'=4,'zt_1'=4,'xy_0'=8,'xy_1'=2] {'zt_1'}, use_global_device_ids=true, to_apply=%region_128.129 | all-reduce | flops 3 | bytes 24 | tf_op jit(solution)/shard_map/psum | solution.py:60
  228.5 15.2 %all-reduce.37 = (f32[1]{0:T(128)}, f32[1]{0:T(128)}, f32[1]{0:T(128)}) all-reduce(f32[1]{0:T(128)} %get-tuple-element.428, f32[1]{0:T(128)} %get-tuple-element.429, f32[1]{0:T(128)} %get-tuple-element.430), channel_id=1, replica_groups=mesh['grp'=2,'zt_0'=4,'zt_1'=4,'xy_0'=8,'xy_1'=2] {'xy_0'}, use_global_device_ids=true, to_apply=%region_129.130 | all-reduce | flops 3 | bytes 24 | tf_op jit(solution)/shard_map/psum | solution.py:60
  243.7 8.9 %all-reduce.58 = (f32[1]{0:T(128)}, f32[1]{0:T(128)}, f32[1]{0:T(128)}) all-reduce(f32[1]{0:T(128)} %get-tuple-element.407, f32[1]{0:T(128)} %get-tuple-element.408, f32[1]{0:T(128)} %get-tuple-element.409), channel_id=1, replica_groups=mesh['grp'=2,'zt_0'=4,'zt_1'=4,'xy_0'=8,'xy_1'=2] {'xy_1'}, use_global_device_ids=true, to_apply=%region_130.131 | all-reduce | flops 3 | bytes 24 | tf_op jit(solution)/shard_map/psum | solution.py:60
  286.6 9.3 %all-reduce.50 = (f32[1]{0:T(128)}, f32[1]{0:T(128)}, f32[1]{0:T(128)}) all-reduce(f32[1]{0:T(128)} %bitcast.269, f32[1]{0:T(128)} %bitcast.273, f32[1]{0:T(128)} %bitcast.274), channel_id=1, replica_groups=mesh['grp'=2,'zt_0'=4,'zt_1'=4,'xy_0'=8,'xy_1'=2] {'zt_0'}, use_global_device_ids=true, to_apply=%region_174.175 | all-reduce | flops 3 | bytes 24 | tf_op jit(solution)/shard_map/psum | solution.py:60
  295.8 10.2 %all-reduce.43 = (f32[1]{0:T(128)}, f32[1]{0:T(128)}, f32[1]{0:T(128)}) all-reduce(f32[1]{0:T(128)} %get-tuple-element.446, f32[1]{0:T(128)} %get-tuple-element.447, f32[1]{0:T(128)} %get-tuple-element.448), channel_id=1, replica_groups=mesh['grp'=2,'zt_0'=4,'zt_1'=4,'xy_0'=8,'xy_1'=2] {'zt_1'}, use_global_device_ids=true, to_apply=%region_175.176 | all-reduce | flops 3 | bytes 24 | tf_op jit(solution)/shard_map/psum | solution.py:60
  306.0 14.6 %all-reduce.36 = (f32[1]{0:T(128)}, f32[1]{0:T(128)}, f32[1]{0:T(128)}) all-reduce(f32[1]{0:T(128)} %get-tuple-element.425, f32[1]{0:T(128)} %get-tuple-element.426, f32[1]{0:T(128)} %get-tuple-element.427), channel_id=1, replica_groups=mesh['grp'=2,'zt_0'=4,'zt_1'=4,'xy_0'=8,'xy_1'=2] {'xy_0'}, use_global_device_ids=true, to_apply=%region_176.177 | all-reduce | flops 3 | bytes 24 | tf_op jit(solution)/shard_map/psum | solution.py:60
  363.7 9.1 %all-reduce.49 = (f32[1]{0:T(128)}, f32[1]{0:T(128)}, f32[1]{0:T(128)}) all-reduce(f32[1]{0:T(128)} %bitcast.334, f32[1]{0:T(128)} %bitcast.338, f32[1]{0:T(128)} %bitcast.339), channel_id=1, replica_groups=mesh['grp'=2,'zt_0'=4,'zt_1'=4,'xy_0'=8,'xy_1'=2] {'zt_0'}, use_global_device_ids=true, to_apply=%region_221.222 | all-reduce | flops 3 | bytes 24 | tf_op jit(solution)/shard_map/psum | solution.py:60
  372.8 10.4 %all-reduce.42 = (f32[1]{0:T(128)}, f32[1]{0:T(128)}, f32[1]{0:T(128)}) all-reduce(f32[1]{0:T(128)} %get-tuple-element.443, f32[1]{0:T(128)} %get-tuple-element.444, f32[1]{0:T(128)} %get-tuple-element.445), channel_id=1, replica_groups=mesh['grp'=2,'zt_0'=4,'zt_1'=4,'xy_0'=8,'xy_1'=2] {'zt_1'}, use_global_device_ids=true, to_apply=%region_222.223 | all-reduce | flops 3 | bytes 24 | tf_op jit(solution)/shard_map/psum | solution.py:60
  383.2 14.6 %all-reduce.35 = (f32[1]{0:T(128)}, f32[1]{0:T(128)}, f32[1]{0:T(128)}) all-reduce(f32[1]{0:T(128)} %get-tuple-element.422, f32[1]{0:T(128)} %get-tuple-element.423, f32[1]{0:T(128)} %get-tuple-element.424), channel_id=1, replica_groups=mesh['grp'=2,'zt_0'=4,'zt_1'=4,'xy_0'=8,'xy_1'=2] {'xy_0'}, use_global_device_ids=true, to_apply=%region_223.224 | all-reduce | flops 3 | bytes 24 | tf_op jit(solution)/shard_map/psum | solution.py:60
  397.8 8.8 %all-reduce.56 = (f32[1]{0:T(128)}, f32[1]{0:T(128)}, f32[1]{0:T(128)}) all-reduce(f32[1]{0:T(128)} %get-tuple-element.401, f32[1]{0:T(128)} %get-tuple-element.402, f32[1]{0:T(128)} %get-tuple-element.403), channel_id=1, replica_groups=mesh['grp'=2,'zt_0'=4,'zt_1'=4,'xy_0'=8,'xy_1'=2] {'xy_1'}, use_global_device_ids=true, to_apply=%region_224.225 | all-reduce | flops 3 | bytes 24 | tf_op jit(solution)/shard_map/psum | solution.py:60
  441.0 9.1 %all-reduce.48 = (f32[1]{0:T(128)}, f32[1]{0:T(128)}, f32[1]{0:T(128)}) all-reduce(f32[1]{0:T(128)} %bitcast.399, f32[1]{0:T(128)} %bitcast.403, f32[1]{0:T(128)} %bitcast.404), channel_id=1, replica_groups=mesh['grp'=2,'zt_0'=4,'zt_1'=4,'xy_0'=8,'xy_1'=2] {'zt_0'}, use_global_device_ids=true, to_apply=%region_268.269 | all-reduce | flops 3 | bytes 24 | tf_op jit(solution)/shard_map/psum | solution.py:60
  450.1 10.3 %all-reduce.41 = (f32[1]{0:T(128)}, f32[1]{0:T(128)}, f32[1]{0:T(128)}) all-reduce(f32[1]{0:T(128)} %get-tuple-element.440, f32[1]{0:T(128)} %get-tuple-element.441, f32[1]{0:T(128)} %get-tuple-element.442), channel_id=1, replica_groups=mesh['grp'=2,'zt_0'=4,'zt_1'=4,'xy_0'=8,'xy_1'=2] {'zt_1'}, use_global_device_ids=true, to_apply=%region_269.270 | all-reduce | flops 3 | bytes 24 | tf_op jit(solution)/shard_map/psum | solution.py:60
  460.4 14.6 %all-reduce.34 = (f32[1]{0:T(128)}, f32[1]{0:T(128)}, f32[1]{0:T(128)}) all-reduce(f32[1]{0:T(128)} %get-tuple-element.419, f32[1]{0:T(128)} %get-tuple-element.420, f32[1]{0:T(128)} %get-tuple-element.421), channel_id=1, replica_groups=mesh['grp'=2,'zt_0'=4,'zt_1'=4,'xy_0'=8,'xy_1'=2] {'xy_0'}, use_global_device_ids=true, to_apply=%region_270.271 | all-reduce | flops 3 | bytes 24 | tf_op jit(solution)/shard_map/psum | solution.py:60
  518.2 9.1 %all-reduce.47 = (f32[1]{0:T(128)}, f32[1]{0:T(128)}, f32[1]{0:T(128)}) all-reduce(f32[1]{0:T(128)} %bitcast.464, f32[1]{0:T(128)} %bitcast.468, f32[1]{0:T(128)} %bitcast.469), channel_id=1, replica_groups=mesh['grp'=2,'zt_0'=4,'zt_1'=4,'xy_0'=8,'xy_1'=2] {'zt_0'}, use_global_device_ids=true, to_apply=%region_315.316 | all-reduce | flops 3 | bytes 24 | tf_op jit(solution)/shard_map/psum | solution.py:60
  527.3 10.4 %all-reduce.40 = (f32[1]{0:T(128)}, f32[1]{0:T(128)}, f32[1]{0:T(128)}) all-reduce(f32[1]{0:T(128)} %get-tuple-element.437, f32[1]{0:T(128)} %get-tuple-element.438, f32[1]{0:T(128)} %get-tuple-element.439), channel_id=1, replica_groups=mesh['grp'=2,'zt_0'=4,'zt_1'=4,'xy_0'=8,'xy_1'=2] {'zt_1'}, use_global_device_ids=true, to_apply=%region_316.317 | all-reduce | flops 3 | bytes 24 | tf_op jit(solution)/shard_map/psum | solution.py:60
  537.7 14.5 %all-reduce.33 = (f32[1]{0:T(128)}, f32[1]{0:T(128)}, f32[1]{0:T(128)}) all-reduce(f32[1]{0:T(128)} %get-tuple-element.416, f32[1]{0:T(128)} %get-tuple-element.417, f32[1]{0:T(128)} %get-tuple-element.418), channel_id=1, replica_groups=mesh['grp'=2,'zt_0'=4,'zt_1'=4,'xy_0'=8,'xy_1'=2] {'xy_0'}, use_global_device_ids=true, to_apply=%region_317.318 | all-reduce | flops 3 | bytes 24 | tf_op jit(solution)/shard_map/psum | solution.py:60
  552.2 8.8 %all-reduce.54 = (f32[1]{0:T(128)}, f32[1]{0:T(128)}, f32[1]{0:T(128)}) all-reduce(f32[1]{0:T(128)} %get-tuple-element.395, f32[1]{0:T(128)} %get-tuple-element.396, f32[1]{0:T(128)} %get-tuple-element.397), channel_id=1, replica_groups=mesh['grp'=2,'zt_0'=4,'zt_1'=4,'xy_0'=8,'xy_1'=2] {'xy_1'}, use_global_device_ids=true, to_apply=%region_318.319 | all-reduce | flops 3 | bytes 24 | tf_op jit(solution)/shard_map/psum | solution.py:60
  595.6 8.9 %psum.747 = f32[1]{0:T(128)} all-reduce(f32[1]{0:T(128)} %bitcast.529), channel_id=1, replica_groups=mesh['grp'=2,'zt_0'=4,'zt_1'=4,'xy_0'=8,'xy_1'=2] {'zt_0'}, use_global_device_ids=true, to_apply=%region_362.363 | all-reduce | flops 1 | bytes 8 | tf_op jit(solution)/shard_map/psum | solution.py:60
  604.5 10.6 %psum.748 = f32[1]{0:T(128)} all-reduce(f32[1]{0:T(128)} %psum.747), channel_id=1, replica_groups=mesh['grp'=2,'zt_0'=4,'zt_1'=4,'xy_0'=8,'xy_1'=2] {'zt_1'}, use_global_device_ids=true, to_apply=%region_363.364 | all-reduce | flops 1 | bytes 8 | tf_op jit(solution)/shard_map/psum | solution.py:60
  615.1 14.5 %psum.749 = f32[1]{0:T(128)} all-reduce(f32[1]{0:T(128)} %psum.748), channel_id=1, replica_groups=mesh['grp'=2,'zt_0'=4,'zt_1'=4,'xy_0'=8,'xy_1'=2] {'xy_0'}, use_global_device_ids=true, to_apply=%region_364.365 | all-reduce | flops 1 | bytes 8 | tf_op jit(solution)/shard_map/psum | solution.py:60
  645.8 9.2 %psum.752 = f32[]{:T(128)} all-reduce(f32[]{:T(128)} %psum.751), channel_id=1, replica_groups=mesh['grp'=2,'zt_0'=4,'zt_1'=4,'xy_0'=8,'xy_1'=2] {'zt_0'}, use_global_device_ids=true, to_apply=%region_369.370 | all-reduce | flops 1 | bytes 8 | tf_op jit(solution)/shard_map/psum | solution.py:60
  655.1 11.3 %psum.753 = f32[]{:T(128)} all-reduce(f32[]{:T(128)} %psum.752), channel_id=1, replica_groups=mesh['grp'=2,'zt_0'=4,'zt_1'=4,'xy_0'=8,'xy_1'=2] {'zt_1'}, use_global_device_ids=true, to_apply=%region_370.371 | all-reduce | flops 1 | bytes 8 | tf_op jit(solution)/shard_map/psum | solution.py:60
  666.4 13.0 %psum.754 = f32[]{:T(128)} all-reduce(f32[]{:T(128)} %psum.753), channel_id=1, replica_groups=mesh['grp'=2,'zt_0'=4,'zt_1'=4,'xy_0'=8,'xy_1'=2] {'xy_0'}, use_global_device_ids=true, to_apply=%region_371.372 | all-reduce | flops 1 | bytes 8 | tf_op jit(solution)/shard_map/psum | solution.py:60
  679.4 12.0 %psum.755 = f32[]{:T(128)} all-reduce(f32[]{:T(128)} %psum.754), channel_id=1, replica_groups=mesh['grp'=2,'zt_0'=4,'zt_1'=4,'xy_0'=8,'xy_1'=2] {'xy_1'}, use_global_device_ids=true, to_apply=%region_372.373 | all-reduce | flops 1 | bytes 8 | tf_op jit(solution)/shard_map/psum | solution.py:60
  (1262 shorter events, 311.2 us)
Async XLA Ops:
  2.4 21.0 %all-to-all-start = ((f32[2,2,2,3,3,2,4,128]{7,5,4,3,2,6,1,0:T(2,128)}), f32[2,2,2,3,3,2,4,128]{7,5,4,3,2,6,1,0:T(2,128)S(1)}, u32[]{:S(2)}, u32[]{:S(2)}) async-start(f32[2,2,2,3,3,2,4,128]{7,5,4,3,2,6,1,0:T(2,128)} %broadcast_in_dim.14), calls=%async_computation | async-start | bytes 589824 | tf_op jit(solution)/shard_map/all_to_all | solution.py:18
  6.2 12.3 %collective-permute-start.2 = (f32[1,2,3,2,1,128]{5,4,3,2,1,0:T(1,128)S(1)}, f32[1,2,3,2,1,128]{5,4,3,2,1,0:T(1,128)S(1)}, u32[]{:S(2)}, u32[]{:S(2)}) collective-permute-start(f32[1,2,3,2,1,128]{5,4,3,2,1,0:T(1,128)S(1)} %get-tuple-element.958), channel_id=1, source_target_pairs={{0,16},{16,32},{32,48},{48,64},{64,80},{80,96},{96,112},{112,128},... | collective-permute-start | bytes 18440 | tf_op jit(solution)/shard_map/ppermute | solution.py:46
  14.8 8.6 %collective-permute-start.5 = (f32[1,2,3,1,4,128]{5,4,3,2,1,0:T(4,128)S(1)}, f32[1,2,3,1,4,128]{5,4,3,2,1,0:T(4,128)S(1)}, u32[]{:S(2)}, u32[]{:S(2)}) collective-permute-start(f32[1,2,3,1,4,128]{5,4,3,2,1,0:T(4,128)S(1)} %get-tuple-element.956), channel_id=1, source_target_pairs={{0,1},{1,2},{2,3},{3,4},{4,5},{5,6},{6,7},{7,8},{8,9},{9,10},{10,1... | collective-permute-start | bytes 36872 | tf_op jit(solution)/shard_map/ppermute | solution.py:46
  33.3 18.2 %collective-permute-start.8 = (f32[1,2,3,1,4,128]{5,4,3,2,1,0:T(4,128)S(1)}, f32[1,2,3,1,4,128]{5,4,3,2,1,0:T(4,128)S(1)}, u32[]{:S(2)}, u32[]{:S(2)}) collective-permute-start(f32[1,2,3,1,4,128]{5,4,3,2,1,0:T(4,128)S(1)} %get-tuple-element.934), channel_id=1, source_target_pairs={{1,0},{2,1},{3,2},{4,3},{5,4},{6,5},{7,6},{8,7},{9,8},{10,9},{11,1... | collective-permute-start | bytes 36872 | tf_op jit(solution)/shard_map/ppermute | solution.py:47
  37.8 13.7 %collective-permute-start.9 = (f32[1,2,3,1,4,128]{5,4,3,2,1,0:T(4,128)S(1)}, f32[1,2,3,1,4,128]{5,4,3,2,1,0:T(4,128)S(1)}, u32[]{:S(2)}, u32[]{:S(2)}) collective-permute-start(f32[1,2,3,1,4,128]{5,4,3,2,1,0:T(4,128)S(1)} %get-tuple-element.933), channel_id=1, source_target_pairs={{0,1},{1,2},{2,3},{3,4},{4,5},{5,6},{6,7},{7,8},{8,9},{9,10},{10,1... | collective-permute-start | bytes 36872 | tf_op jit(solution)/shard_map/ppermute | solution.py:46
  37.8 8.4 %collective-permute-start.6 = (f32[1,2,3,2,1,128]{5,4,3,2,1,0:T(1,128)S(1)}, f32[1,2,3,2,1,128]{5,4,3,2,1,0:T(1,128)S(1)}, u32[]{:S(2)}, u32[]{:S(2)}) collective-permute-start(f32[1,2,3,2,1,128]{5,4,3,2,1,0:T(1,128)S(1)} %get-tuple-element.944), channel_id=1, source_target_pairs={{0,16},{16,32},{32,48},{48,64},{64,80},{80,96},{96,112},{112,128},... | collective-permute-start | bytes 18440 | tf_op jit(solution)/shard_map/ppermute | solution.py:46
  99.9 9.4 %collective-permute-start.10 = (f32[1,2,3,2,1,128]{5,4,3,2,1,0:T(1,128)S(1)}, f32[1,2,3,2,1,128]{5,4,3,2,1,0:T(1,128)S(1)}, u32[]{:S(2)}, u32[]{:S(2)}) collective-permute-start(f32[1,2,3,2,1,128]{5,4,3,2,1,0:T(1,128)S(1)} %get-tuple-element.929), channel_id=1, source_target_pairs={{0,16},{16,32},{32,48},{48,64},{64,80},{80,96},{96,112},{112,128},... | collective-permute-start | bytes 18440 | tf_op jit(solution)/shard_map/ppermute | solution.py:46
  115.2 14.9 %collective-permute-start.16 = (f32[1,2,3,1,4,128]{5,4,3,2,1,0:T(4,128)S(1)}, f32[1,2,3,1,4,128]{5,4,3,2,1,0:T(4,128)S(1)}, u32[]{:S(2)}, u32[]{:S(2)}) collective-permute-start(f32[1,2,3,1,4,128]{5,4,3,2,1,0:T(4,128)S(1)} %get-tuple-element.907), channel_id=1, source_target_pairs={{1,0},{2,1},{3,2},{4,3},{5,4},{6,5},{7,6},{8,7},{9,8},{10,9},{11,1... | collective-permute-start | bytes 36872 | tf_op jit(solution)/shard_map/ppermute | solution.py:47
  116.9 13.2 %collective-permute-start.17 = (f32[1,2,3,1,4,128]{5,4,3,2,1,0:T(4,128)S(1)}, f32[1,2,3,1,4,128]{5,4,3,2,1,0:T(4,128)S(1)}, u32[]{:S(2)}, u32[]{:S(2)}) collective-permute-start(f32[1,2,3,1,4,128]{5,4,3,2,1,0:T(4,128)S(1)} %get-tuple-element.906), channel_id=1, source_target_pairs={{0,1},{1,2},{2,3},{3,4},{4,5},{5,6},{6,7},{7,8},{8,9},{9,10},{10,1... | collective-permute-start | bytes 36872 | tf_op jit(solution)/shard_map/ppermute | solution.py:46
  121.2 7.7 %collective-permute-start.15 = (f32[1,2,3,2,1,128]{5,4,3,2,1,0:T(1,128)S(1)}, f32[1,2,3,2,1,128]{5,4,3,2,1,0:T(1,128)S(1)}, u32[]{:S(2)}, u32[]{:S(2)}) collective-permute-start(f32[1,2,3,2,1,128]{5,4,3,2,1,0:T(1,128)S(1)} %get-tuple-element.916), channel_id=1, source_target_pairs={{16,0},{32,16},{48,32},{64,48},{80,64},{96,80},{112,96},{128,112},... | collective-permute-start | bytes 18440 | tf_op jit(solution)/shard_map/ppermute | solution.py:47
  176.9 10.6 %collective-permute-start.18 = (f32[1,2,3,2,1,128]{5,4,3,2,1,0:T(1,128)S(1)}, f32[1,2,3,2,1,128]{5,4,3,2,1,0:T(1,128)S(1)}, u32[]{:S(2)}, u32[]{:S(2)}) collective-permute-start(f32[1,2,3,2,1,128]{5,4,3,2,1,0:T(1,128)S(1)} %get-tuple-element.902), channel_id=1, source_target_pairs={{0,16},{16,32},{32,48},{48,64},{64,80},{80,96},{96,112},{112,128},... | collective-permute-start | bytes 18440 | tf_op jit(solution)/shard_map/ppermute | solution.py:46
  192.1 15.2 %collective-permute-start.24 = (f32[1,2,3,1,4,128]{5,4,3,2,1,0:T(4,128)S(1)}, f32[1,2,3,1,4,128]{5,4,3,2,1,0:T(4,128)S(1)}, u32[]{:S(2)}, u32[]{:S(2)}) collective-permute-start(f32[1,2,3,1,4,128]{5,4,3,2,1,0:T(4,128)S(1)} %get-tuple-element.880), channel_id=1, source_target_pairs={{1,0},{2,1},{3,2},{4,3},{5,4},{6,5},{7,6},{8,7},{9,8},{10,9},{11,1... | collective-permute-start | bytes 36872 | tf_op jit(solution)/shard_map/ppermute | solution.py:47
  193.9 13.5 %collective-permute-start.25 = (f32[1,2,3,1,4,128]{5,4,3,2,1,0:T(4,128)S(1)}, f32[1,2,3,1,4,128]{5,4,3,2,1,0:T(4,128)S(1)}, u32[]{:S(2)}, u32[]{:S(2)}) collective-permute-start(f32[1,2,3,1,4,128]{5,4,3,2,1,0:T(4,128)S(1)} %get-tuple-element.879), channel_id=1, source_target_pairs={{0,1},{1,2},{2,3},{3,4},{4,5},{5,6},{6,7},{7,8},{8,9},{9,10},{10,1... | collective-permute-start | bytes 36872 | tf_op jit(solution)/shard_map/ppermute | solution.py:46
  198.6 7.7 %collective-permute-start.23 = (f32[1,2,3,2,1,128]{5,4,3,2,1,0:T(1,128)S(1)}, f32[1,2,3,2,1,128]{5,4,3,2,1,0:T(1,128)S(1)}, u32[]{:S(2)}, u32[]{:S(2)}) collective-permute-start(f32[1,2,3,2,1,128]{5,4,3,2,1,0:T(1,128)S(1)} %get-tuple-element.889), channel_id=1, source_target_pairs={{16,0},{32,16},{48,32},{64,48},{80,64},{96,80},{112,96},{128,112},... | collective-permute-start | bytes 18440 | tf_op jit(solution)/shard_map/ppermute | solution.py:47
  255.1 9.5 %collective-permute-start.26 = (f32[1,2,3,2,1,128]{5,4,3,2,1,0:T(1,128)S(1)}, f32[1,2,3,2,1,128]{5,4,3,2,1,0:T(1,128)S(1)}, u32[]{:S(2)}, u32[]{:S(2)}) collective-permute-start(f32[1,2,3,2,1,128]{5,4,3,2,1,0:T(1,128)S(1)} %get-tuple-element.875), channel_id=1, source_target_pairs={{0,16},{16,32},{32,48},{48,64},{64,80},{80,96},{96,112},{112,128},... | collective-permute-start | bytes 18440 | tf_op jit(solution)/shard_map/ppermute | solution.py:46
  270.3 14.9 %collective-permute-start.32 = (f32[1,2,3,1,4,128]{5,4,3,2,1,0:T(4,128)S(1)}, f32[1,2,3,1,4,128]{5,4,3,2,1,0:T(4,128)S(1)}, u32[]{:S(2)}, u32[]{:S(2)}) collective-permute-start(f32[1,2,3,1,4,128]{5,4,3,2,1,0:T(4,128)S(1)} %get-tuple-element.853), channel_id=1, source_target_pairs={{1,0},{2,1},{3,2},{4,3},{5,4},{6,5},{7,6},{8,7},{9,8},{10,9},{11,1... | collective-permute-start | bytes 36872 | tf_op jit(solution)/shard_map/ppermute | solution.py:47
  272.1 13.2 %collective-permute-start.33 = (f32[1,2,3,1,4,128]{5,4,3,2,1,0:T(4,128)S(1)}, f32[1,2,3,1,4,128]{5,4,3,2,1,0:T(4,128)S(1)}, u32[]{:S(2)}, u32[]{:S(2)}) collective-permute-start(f32[1,2,3,1,4,128]{5,4,3,2,1,0:T(4,128)S(1)} %get-tuple-element.852), channel_id=1, source_target_pairs={{0,1},{1,2},{2,3},{3,4},{4,5},{5,6},{6,7},{7,8},{8,9},{9,10},{10,1... | collective-permute-start | bytes 36872 | tf_op jit(solution)/shard_map/ppermute | solution.py:46
  276.4 7.7 %collective-permute-start.31 = (f32[1,2,3,2,1,128]{5,4,3,2,1,0:T(1,128)S(1)}, f32[1,2,3,2,1,128]{5,4,3,2,1,0:T(1,128)S(1)}, u32[]{:S(2)}, u32[]{:S(2)}) collective-permute-start(f32[1,2,3,2,1,128]{5,4,3,2,1,0:T(1,128)S(1)} %get-tuple-element.862), channel_id=1, source_target_pairs={{16,0},{32,16},{48,32},{64,48},{80,64},{96,80},{112,96},{128,112},... | collective-permute-start | bytes 18440 | tf_op jit(solution)/shard_map/ppermute | solution.py:47
  331.9 9.8 %collective-permute-start.34 = (f32[1,2,3,2,1,128]{5,4,3,2,1,0:T(1,128)S(1)}, f32[1,2,3,2,1,128]{5,4,3,2,1,0:T(1,128)S(1)}, u32[]{:S(2)}, u32[]{:S(2)}) collective-permute-start(f32[1,2,3,2,1,128]{5,4,3,2,1,0:T(1,128)S(1)} %get-tuple-element.848), channel_id=1, source_target_pairs={{0,16},{16,32},{32,48},{48,64},{64,80},{80,96},{96,112},{112,128},... | collective-permute-start | bytes 18440 | tf_op jit(solution)/shard_map/ppermute | solution.py:46
  347.1 15.2 %collective-permute-start.40 = (f32[1,2,3,1,4,128]{5,4,3,2,1,0:T(4,128)S(1)}, f32[1,2,3,1,4,128]{5,4,3,2,1,0:T(4,128)S(1)}, u32[]{:S(2)}, u32[]{:S(2)}) collective-permute-start(f32[1,2,3,1,4,128]{5,4,3,2,1,0:T(4,128)S(1)} %get-tuple-element.826), channel_id=1, source_target_pairs={{1,0},{2,1},{3,2},{4,3},{5,4},{6,5},{7,6},{8,7},{9,8},{10,9},{11,1... | collective-permute-start | bytes 36872 | tf_op jit(solution)/shard_map/ppermute | solution.py:47
  348.9 13.5 %collective-permute-start.41 = (f32[1,2,3,1,4,128]{5,4,3,2,1,0:T(4,128)S(1)}, f32[1,2,3,1,4,128]{5,4,3,2,1,0:T(4,128)S(1)}, u32[]{:S(2)}, u32[]{:S(2)}) collective-permute-start(f32[1,2,3,1,4,128]{5,4,3,2,1,0:T(4,128)S(1)} %get-tuple-element.825), channel_id=1, source_target_pairs={{0,1},{1,2},{2,3},{3,4},{4,5},{5,6},{6,7},{7,8},{8,9},{9,10},{10,1... | collective-permute-start | bytes 36872 | tf_op jit(solution)/shard_map/ppermute | solution.py:46
  353.5 7.7 %collective-permute-start.39 = (f32[1,2,3,2,1,128]{5,4,3,2,1,0:T(1,128)S(1)}, f32[1,2,3,2,1,128]{5,4,3,2,1,0:T(1,128)S(1)}, u32[]{:S(2)}, u32[]{:S(2)}) collective-permute-start(f32[1,2,3,2,1,128]{5,4,3,2,1,0:T(1,128)S(1)} %get-tuple-element.835), channel_id=1, source_target_pairs={{16,0},{32,16},{48,32},{64,48},{80,64},{96,80},{112,96},{128,112},... | collective-permute-start | bytes 18440 | tf_op jit(solution)/shard_map/ppermute | solution.py:47
  409.2 9.8 %collective-permute-start.42 = (f32[1,2,3,2,1,128]{5,4,3,2,1,0:T(1,128)S(1)}, f32[1,2,3,2,1,128]{5,4,3,2,1,0:T(1,128)S(1)}, u32[]{:S(2)}, u32[]{:S(2)}) collective-permute-start(f32[1,2,3,2,1,128]{5,4,3,2,1,0:T(1,128)S(1)} %get-tuple-element.821), channel_id=1, source_target_pairs={{0,16},{16,32},{32,48},{48,64},{64,80},{80,96},{96,112},{112,128},... | collective-permute-start | bytes 18440 | tf_op jit(solution)/shard_map/ppermute | solution.py:46
  424.5 15.2 %collective-permute-start.48 = (f32[1,2,3,1,4,128]{5,4,3,2,1,0:T(4,128)S(1)}, f32[1,2,3,1,4,128]{5,4,3,2,1,0:T(4,128)S(1)}, u32[]{:S(2)}, u32[]{:S(2)}) collective-permute-start(f32[1,2,3,1,4,128]{5,4,3,2,1,0:T(4,128)S(1)} %get-tuple-element.799), channel_id=1, source_target_pairs={{1,0},{2,1},{3,2},{4,3},{5,4},{6,5},{7,6},{8,7},{9,8},{10,9},{11,1... | collective-permute-start | bytes 36872 | tf_op jit(solution)/shard_map/ppermute | solution.py:47
  426.2 13.5 %collective-permute-start.49 = (f32[1,2,3,1,4,128]{5,4,3,2,1,0:T(4,128)S(1)}, f32[1,2,3,1,4,128]{5,4,3,2,1,0:T(4,128)S(1)}, u32[]{:S(2)}, u32[]{:S(2)}) collective-permute-start(f32[1,2,3,1,4,128]{5,4,3,2,1,0:T(4,128)S(1)} %get-tuple-element.798), channel_id=1, source_target_pairs={{0,1},{1,2},{2,3},{3,4},{4,5},{5,6},{6,7},{7,8},{8,9},{9,10},{10,1... | collective-permute-start | bytes 36872 | tf_op jit(solution)/shard_map/ppermute | solution.py:46
  486.4 9.7 %collective-permute-start.50 = (f32[1,2,3,2,1,128]{5,4,3,2,1,0:T(1,128)S(1)}, f32[1,2,3,2,1,128]{5,4,3,2,1,0:T(1,128)S(1)}, u32[]{:S(2)}, u32[]{:S(2)}) collective-permute-start(f32[1,2,3,2,1,128]{5,4,3,2,1,0:T(1,128)S(1)} %get-tuple-element.794), channel_id=1, source_target_pairs={{0,16},{16,32},{32,48},{48,64},{64,80},{80,96},{96,112},{112,128},... | collective-permute-start | bytes 18440 | tf_op jit(solution)/shard_map/ppermute | solution.py:46
  501.7 15.2 %collective-permute-start.56 = (f32[1,2,3,1,4,128]{5,4,3,2,1,0:T(4,128)S(1)}, f32[1,2,3,1,4,128]{5,4,3,2,1,0:T(4,128)S(1)}, u32[]{:S(2)}, u32[]{:S(2)}) collective-permute-start(f32[1,2,3,1,4,128]{5,4,3,2,1,0:T(4,128)S(1)} %get-tuple-element.772), channel_id=1, source_target_pairs={{1,0},{2,1},{3,2},{4,3},{5,4},{6,5},{7,6},{8,7},{9,8},{10,9},{11,1... | collective-permute-start | bytes 36872 | tf_op jit(solution)/shard_map/ppermute | solution.py:47
  503.4 13.5 %collective-permute-start.57 = (f32[1,2,3,1,4,128]{5,4,3,2,1,0:T(4,128)S(1)}, f32[1,2,3,1,4,128]{5,4,3,2,1,0:T(4,128)S(1)}, u32[]{:S(2)}, u32[]{:S(2)}) collective-permute-start(f32[1,2,3,1,4,128]{5,4,3,2,1,0:T(4,128)S(1)} %get-tuple-element.771), channel_id=1, source_target_pairs={{0,1},{1,2},{2,3},{3,4},{4,5},{5,6},{6,7},{7,8},{8,9},{9,10},{10,1... | collective-permute-start | bytes 36872 | tf_op jit(solution)/shard_map/ppermute | solution.py:46
  563.7 10.0 %collective-permute-start.58 = (f32[1,2,3,2,1,128]{5,4,3,2,1,0:T(1,128)S(1)}, f32[1,2,3,2,1,128]{5,4,3,2,1,0:T(1,128)S(1)}, u32[]{:S(2)}, u32[]{:S(2)}) collective-permute-start(f32[1,2,3,2,1,128]{5,4,3,2,1,0:T(1,128)S(1)} %get-tuple-element.767), channel_id=1, source_target_pairs={{0,16},{16,32},{32,48},{48,64},{64,80},{80,96},{96,112},{112,128},... | collective-permute-start | bytes 18440 | tf_op jit(solution)/shard_map/ppermute | solution.py:46
  579.0 15.4 %collective-permute-start.64 = (f32[1,2,3,1,4,128]{5,4,3,2,1,0:T(4,128)S(1)}, f32[1,2,3,1,4,128]{5,4,3,2,1,0:T(4,128)S(1)}, u32[]{:S(2)}, u32[]{:S(2)}) collective-permute-start(f32[1,2,3,1,4,128]{5,4,3,2,1,0:T(4,128)S(1)} %get-tuple-element.745), channel_id=1, source_target_pairs={{1,0},{2,1},{3,2},{4,3},{5,4},{6,5},{7,6},{8,7},{9,8},{10,9},{11,1... | collective-permute-start | bytes 36872 | tf_op jit(solution)/shard_map/ppermute | solution.py:47
  580.7 13.6 %collective-permute-start.65 = (f32[1,2,3,1,4,128]{5,4,3,2,1,0:T(4,128)S(1)}, f32[1,2,3,1,4,128]{5,4,3,2,1,0:T(4,128)S(1)}, u32[]{:S(2)}, u32[]{:S(2)}) collective-permute-start(f32[1,2,3,1,4,128]{5,4,3,2,1,0:T(4,128)S(1)} %get-tuple-element.744), channel_id=1, source_target_pairs={{0,1},{1,2},{2,3},{3,4},{4,5},{5,6},{6,7},{7,8},{8,9},{9,10},{10,1... | collective-permute-start | bytes 36872 | tf_op jit(solution)/shard_map/ppermute | solution.py:46
  585.4 7.8 %collective-permute-start.63 = (f32[1,2,3,2,1,128]{5,4,3,2,1,0:T(1,128)S(1)}, f32[1,2,3,2,1,128]{5,4,3,2,1,0:T(1,128)S(1)}, u32[]{:S(2)}, u32[]{:S(2)}) collective-permute-start(f32[1,2,3,2,1,128]{5,4,3,2,1,0:T(1,128)S(1)} %get-tuple-element.754), channel_id=1, source_target_pairs={{16,0},{32,16},{48,32},{64,48},{80,64},{96,80},{112,96},{128,112},... | collective-permute-start | bytes 18440 | tf_op jit(solution)/shard_map/ppermute | solution.py:47
  (39 other events, 221.9 us)
where the time goes:
time: 704 us; the launch traced here: 694 us
  blocking collectives  393 us (56%)
  starting transfers between devices  165 us (23%)
  waiting for transfers between devices  52.8 us (8%)
  local copies, waits for them, and re-layouts  29.3 us (4%)
  between operations  27.1 us (4%)
  other arithmetic  25.8 us (4%)
    psum x37, blocking collectives, one_axis_at_a_time(): x = lax.psum(x, axis)  393 us
    ppermute x32, starting transfers between devices, extended(): lax.ppermute(last, axis, up)  93.9 us
    ppermute x32, starting transfers between devices, extended(): lax.ppermute(initial, axis, [(b, a) for a, b in up])  62.1 us
    ppermute x32, waiting for transfers between devices, extended(): lax.ppermute(initial, axis, [(b, a) for a, b in up])  47.6 us
  transfers between devices with their start and end apart: 67, of which 17 were waited for; matrix products, arithmetic and copies ran while one was open for 3% of the time, Pallas kernels for 0%

commit v1 on v0

v1 whole, which is shorter than its diff:
```python
import functools

import jax
import jax.numpy as jnp
from jax import lax
from jax.experimental import pallas as pl
from jax.experimental.pallas import tpu as pltpu
from jax.sharding import Mesh
from jax.sharding import PartitionSpec as P

NY = 2
NZ = 64
LANES = NY * NZ
STEP = 4
XY = ("xy_0", "xy_1")
ZT = ("zt_0", "zt_1")
ZT_XY = ("zt_0", "zt_1", "xy_0", "xy_1")
F32 = jnp.float32
ROWS = 16
LX_N, L_N = 5, 4


def two_sum(a, b):
    s = a + b
    t = s - a
    return s, (a - (s - t)) + (b - t)


def quick_sum(a, b):
    s = a + b
    return s, b - (s - a)


def halves(a):
    t = a * 4097.0
    h = t - (t - a)
    return h, a - h


def two_prod(a, b):
    p = a * b
    ah, al = halves(a)
    bh, bl = halves(b)
    return p, ((ah * bh - p) + ah * bl + al * bh) + al * bl


@jax.tree_util.register_pytree_node_class
class Pair:
    def __init__(self, h, l):
        self.h = h
        self.l = l

    def tree_flatten(self):
        return (self.h, self.l), None

    @classmethod
    def tree_unflatten(cls, _, leaves):
        return cls(*leaves)

    def __add__(self, o):
        a, e = two_sum(self.h, o.h)
        t, f = two_sum(self.l, o.l)
        a, e = quick_sum(a, e + t)
        return Pair(*quick_sum(a, e + f))

    def __neg__(self):
        return Pair(-self.h, -self.l)

    def __sub__(self, o):
        return self + (-o)

    def __mul__(self, o):
        p, e = two_prod(self.h, o.h)
        return Pair(*quick_sum(p, e + (self.h * o.l + self.l * o.h)))

    def times(self, f):
        p, e = two_prod(self.h, f)
        return Pair(*quick_sum(p, e + self.l * f))

    def __truediv__(self, o):
        q1 = self.h / o.h
        r = self - o.times(q1)
        q2 = r.h / o.h
        r = r - o.times(q2)
        a, b = quick_sum(q1, q2)
        return Pair(*quick_sum(a, b + r.h / o.h))


def plus(a, b):
    return b if a is None else a + b


def run_steps(first, moments, state, m2, one, shifts, final):
    size = STEP
    al, be, c, gam = (dict(state[n]) for n in ("al", "be", "c", "gam"))
    coef = dict(state["coef"])
    part, sol = dict(state["part"]), dict(state["sol"])
    zeta, zeta_old, zeta_new = state["zeta"], state["zeta_old"], state["zeta_new"]
    unit = Pair(one, jnp.zeros_like(one))
    table = {first: list(moments)}
    raised = {}
    if first:
        inv, own, low = {}, {}, {}
        for k in range(first):
            inv[k] = unit / al[k]
            own[k] = (unit + c[k] if k else unit) * inv[k] - m2
            if k:
                low[k] = c[k] * inv[k]
            table[k] = [None] * (2 * size)
        for i in range(1, 2 * size):
            for k in range(first - 1, -1, -1):
                if i < first - k:
                    continue
                t = None
                if table[k][i - 1] is not None:
                    t = plus(t, own[k] * table[k][i - 1])
                if table[k + 1][i - 1] is not None:
                    t = plus(t, -(inv[k] * table[k + 1][i - 1]))
                if k and table[k - 1][i - 1] is not None:
                    t = plus(t, -(low[k] * table[k - 1][i - 1]))
                table[k][i] = t
        rest, top = state["handover"]
        scale = one / top
        for k in range(first - 1):
            raised[k] = {k + 1: one}
        raised[first - 1] = {j: -(rest[j] * scale) for j in rest}
        raised[first - 1][first] = scale
    for i in range(size - 1):
        raised[first + i] = {first + i + 1: one}
    coef[first] = {first: one}
    lead, second = unit, None
    handover = None
    for d in range(size):
        k = first + d
        norm = lead * table[k][d]
        high = lead * table[k][d + 1]
        if second is not None:
            high = high + second * table[k][d]
        gam[k] = norm
        if k == 0:
            part = {0: jnp.ones_like(shifts)}
        else:
            ratio = norm / gam[k - 1]
            be[k - 1] = ratio
            step = zeta_new / zeta
            keep = ratio.h * step * step
            grown = {}
            for j in sorted(set(part) | set(coef[k])):
                t = None
                if j in coef[k]:
                    t = zeta_new * coef[k][j]
                if j in part:
                    t = plus(t, keep * part[j])
                grown[j] = t
            part = grown
            zeta_old, zeta = zeta, zeta_new
        curve = m2 * norm + high
        if k:
            curve = curve - ratio * norm / al[k - 1]
        a = norm / curve
        al[k] = a
        if k:
            a_old, b_old = al[k - 1].h, be[k - 1].h
            zeta_new = (
                zeta
                * zeta_old
                * a_old
                / (a.h * b_old * (zeta_old - zeta) + zeta_old * a_old * (1.0 + shifts * a.h))
            )
            c[k] = a * be[k - 1] / al[k - 1]
            keep_r = unit + c[k]
        else:
            zeta_new = zeta / (1.0 + shifts * a.h)
            keep_r = unit
        gain = a.h * zeta_new / zeta
        for j in part:
            sol[j] = plus(sol.get(j), gain * part[j])
        if d == size - 1 and final:
            break
        image = {}
        for j, v in coef[k].items():
            image[j] = plus(image.get(j), m2.h * v)
            if j == first + size - 1:
                continue
            for jj, w in raised[j].items():
                image[jj] = plus(image.get(jj), w * v)
        following = {}
        for j in sorted(set(coef[k]) | set(image) | set(coef.get(k - 1, {}))):
            t = None
            if j in coef[k]:
                t = keep_r.h * coef[k][j]
            if j in image:
                t = plus(t, -(a.h * image[j]))
            if k and j in coef[k - 1]:
                t = plus(t, -(c[k].h * coef[k - 1][j]))
            following[j] = t
        if d == size - 1:
            handover = (following, -(a.h * coef[k][first + size - 1]))
            break
        coef[k + 1] = following
        row = [None] * (2 * size)
        for i in range(2 * size - 1 - d):
            if table[k][i] is None or table[k][i + 1] is None:
                continue
            t = keep_r * table[k][i] - a * (m2 * table[k][i] + table[k][i + 1])
            if k and table[k - 1][i] is not None:
                t = t - c[k] * table[k - 1][i]
            row[i] = t
        table[k + 1] = row
        image_second = m2 * lead if second is None else m2 * lead + second
        lead, second = -(a * lead), keep_r * lead - a * image_second
    last = first + size - 1
    return {
        "al": al,
        "be": be,
        "c": c,
        "gam": {last: gam[last]},
        "coef": {last: coef[last]},
        "part": part,
        "sol": sol,
        "zeta": zeta,
        "zeta_old": zeta_old,
        "zeta_new": zeta_new,
        "handover": handover,
    }


def start_state(one):
    return {
        "al": {},
        "be": {},
        "c": {},
        "gam": {},
        "coef": {},
        "part": {},
        "sol": {},
        "zeta": one,
        "zeta_old": one,
        "zeta_new": one,
        "handover": None,
    }


def first_state(moments, m2, shifts):
    one = jnp.ones_like(shifts)
    return run_steps(0, moments, start_state(one), m2, one, shifts, False)


def state_shape():
    s = jax.ShapeDtypeStruct((8, LANES), F32)
    moments = [Pair(s, s)] * (2 * STEP)
    out = jax.eval_shape(first_state, moments, Pair(s, s), s)
    return jax.tree_util.tree_flatten(out)


def summed_moments(gathered):
    rows = gathered.shape[0] // 8
    zero = jnp.zeros((8, LANES), F32)
    terms = [Pair(gathered[8 * i : 8 * i + 8], zero) for i in range(rows)]
    while len(terms) > 1:
        terms = [terms[i] + terms[i + 1] for i in range(0, len(terms) - 1, 2)] + (
            [terms[-1]] if len(terms) % 2 else []
        )
    t = terms[0]
    for s in (4, 2, 1):
        t = t + Pair(pltpu.roll(t.h, s, 0), pltpu.roll(t.l, s, 0))
    width = LANES // (2 * STEP)
    s = width // 2
    while s:
        t = t + Pair(pltpu.roll(t.h, LANES - s, 1), pltpu.roll(t.l, LANES - s, 1))
        s //= 2
    lane = lax.broadcasted_iota(jnp.int32, (8, LANES), 1)

    def spread(v, j):
        picked = jnp.where(lane == width * j, v, 0.0)
        return jnp.broadcast_to(jnp.sum(picked, axis=1, keepdims=True), (8, LANES))

    return [Pair(spread(t.h, j), spread(t.l, j)) for j in range(2 * STEP)]


def vm(n):
    return [pl.BlockSpec(memory_space=pltpu.VMEM)] * n


def call(body, name, outs, args, smem=0, scratch=()):
    specs = [pl.BlockSpec(memory_space=pltpu.SMEM)] * smem + vm(len(args) - smem)
    return pl.pallas_call(
        body,
        name=name,
        in_specs=specs,
        out_specs=vm(len(outs)),
        out_shape=[jax.ShapeDtypeStruct(s, F32) for s in outs],
        scratch_shapes=list(scratch),
        compiler_params=pltpu.CompilerParams(vmem_limit_bytes=24 * 1024 * 1024),
    )(*args)


def fold_kernel(where, own, other, source, out):
    first = where[0] == 0
    edge = jnp.where(where[1] == 1, -1.0, 1.0).astype(F32)
    xs, ts = source.shape[3], source.shape[4]
    shape = (ts, LANES)
    lane = lax.broadcasted_iota(jnp.int32, shape, 1)
    row = lax.broadcasted_iota(jnp.int32, shape, 0)
    y = lane // NZ
    yz = y + lane % NZ
    for x in range(xs):
        signs = [
            jnp.full(shape, 0.5, F32),
            jnp.full(shape, 0.5 if x % 2 == 0 else -0.5, F32),
            jnp.where((y + x) % 2 == 0, 0.5, -0.5).astype(F32),
            jnp.where((yz + x) % 2 == 0, 0.5, -0.5).astype(F32)
            * jnp.where(row == ts - 1, edge, 1.0),
        ]
        for mu in range(4):
            for k in range(18):
                p, r, c = k // 9, (k // 3) % 3, k % 3
                a = own[mu % 2, p, r, c, x]
                b = other[mu % 2, p, r, c, x]
                w = jnp.where(first, a, b) if mu < 2 else jnp.where(first, b, a)
                out[18 * mu + k, x] = w * signs[mu]
        for k in range(6):
            out[72 + k, x] = source[0, k // 3, k % 3, x]


def widen(out, index, low, own, high):
    ts = own.shape[0]
    out[(*index, slice(0, ts))] = low
    out[(*index, slice(ts, 2 * ts))] = own
    out[(*index, slice(2 * ts, 3 * ts))] = high
    out[(*index, slice(3 * ts, ROWS))] = jnp.zeros((ROWS - 3 * ts, LANES), F32)


def wide_links_kernel(own, low, high, out, up, down):
    n = own.shape[0]

    def one(k, _):
        for x in range(2):
            widen(out, (k, x), low[k, x], own[k, x], high[k, x])
        return 0

    lax.fori_loop(0, n, one, 0)

    def copy(k, _):
        up[k] = out[k, 1]
        down[k] = out[k, 0]
        return 0

    lax.fori_loop(0, 72, copy, 0)
    for k in range(18):
        up[72 + k] = out[k, 0]
    for k in range(6):
        for x in range(2):
            up[90 + 2 * k + x] = out[72 + k, x]
            down[72 + 2 * k + x] = out[72 + k, x]


def wide_field_kernel(own, low, high, out):
    for k in range(6):
        for x in range(2):
            widen(out, (k, x), low[k, x], own[k, x], high[k, x])


def lanes_of(shape):
    return lax.broadcasted_iota(jnp.int32, shape, 1) % NZ


def z_ahead(v, vy, z):
    return jnp.where(z == NZ - 1, pltpu.roll(vy, LANES - 1, 1), pltpu.roll(v, LANES - 1, 1))


def z_behind(v, vy, z):
    return jnp.where(z == 0, pltpu.roll(vy, 1, 1), pltpu.roll(v, 1, 1))


def times(acc, link, v):
    for r in range(3):
        for c in range(3):
            re, im = link(3 * r + c), link(9 + 3 * r + c)
            acc[r] = acc[r] + re * v[c] - im * v[3 + c]
            acc[3 + r] = acc[3 + r] + re * v[3 + c] + im * v[c]


def less_adjoint(acc, link, v):
    for r in range(3):
        for c in range(3):
            re, im = link(3 * c + r), link(9 + 3 * c + r)
            acc[r] = acc[r] - re * v[c] - im * v[3 + c]
            acc[3 + r] = acc[3 + r] - re * v[3 + c] + im * v[c]


def hop(src, dst, rows, base, links):
    lx, ly, lz, lzb, lt, ltb = links
    z = lanes_of((ROWS, LANES))

    def one(i, _):
        acc = [jnp.zeros((ROWS, LANES), F32)] * 6
        s = base + i
        times(acc, lambda k: lx[k, s + 1], [src[k, i + 2] for k in range(6)])
        less_adjoint(acc, lambda k: lx[k, s], [src[k, i] for k in range(6)])
        v = [src[k, i + 1] for k in range(6)]
        times(acc, lambda k: lt[k, s], [pltpu.roll(u, ROWS - 1, 0) for u in v])
        less_adjoint(acc, lambda k: ltb[k, s], [pltpu.roll(u, 1, 0) for u in v])
        vy = [pltpu.roll(u, NZ, 1) for u in v]
        times(acc, lambda k: ly[k, s], vy)
        times(acc, lambda k: lz[k, s], [z_ahead(u, w, z) for u, w in zip(v, vy)])
        less_adjoint(acc, lambda k: lzb[k, s], [z_behind(u, w, z) for u, w in zip(v, vy)])
        for k in range(6):
            dst[k, i] = acc[k]
        return 0

    lax.fori_loop(0, rows, one, 0)


def norm_row(src, x0, moments, j):
    row = lax.broadcasted_iota(jnp.int32, (8, LANES), 0)
    t = jnp.zeros((8, LANES), F32)
    for k in range(6):
        for x in range(2):
            v = src[k, x0 + x, 0:8]
            t = t + v * v
    t = jnp.sum(jnp.where(row >= 4, t, 0.0), axis=0, keepdims=True)
    return jnp.where(row == j, jnp.broadcast_to(t, (8, LANES)), moments)


def build_links(own, low, high, links):
    lx, ly, lz, lzb, lt, ltb = links
    z = lanes_of((ROWS, LANES))
    for k in range(18):
        lx[k, 0] = low[72 + k]
        lx[k, 1] = low[k]
        lx[k, 2] = own[k, 0]
        lx[k, 3] = own[k, 1]
        lx[k, 4] = high[k]

    for i in range(4):

        def at(k, i=i):
            return low[k] if i == 0 else high[k] if i == 3 else own[k, i - 1]

        for r in range(3):
            for c in range(3):
                k, a = 3 * r + c, 3 * c + r
                ly[k, i] = at(18 + k) - pltpu.roll(at(18 + a), NZ, 1)
                ly[9 + k, i] = at(27 + k) + pltpu.roll(at(27 + a), NZ, 1)
        for k in range(18):
            w = at(36 + k)
            lz[k, i] = w
            lzb[k, i] = z_behind(w, pltpu.roll(w, NZ, 1), z)
            w = at(54 + k)
            lt[k, i] = w
            ltb[k, i] = pltpu.roll(w, 1, 0)


def first_hops_kernel(own, low, high, out, moments, lx, ly, lz, lzb, lt, ltb, v0, v1):
    links = (lx, ly, lz, lzb, lt, ltb)
    build_links(own, low, high, links)
    for k in range(6):
        for x in range(2):
            v0[k, x] = low[90 + 2 * k + x]
            v0[k, 2 + x] = own[72 + k, x]
            v0[k, 4 + x] = high[72 + 2 * k + x]
    hop(v0, v1, 4, 0, links)
    hop(v1, out, 2, 1, links)
    m = norm_row(v0, 2, jnp.zeros((8, LANES), F32), 0)
    m = norm_row(v1, 1, m, 1)
    moments[...] = norm_row(out, 0, m, 2)


def message_row(m):
    s = LANES // 2
    while s >= LANES // (2 * STEP):
        m = m + pltpu.roll(m, s, 1)
        s //= 2
    row = lax.broadcasted_iota(jnp.int32, (8, LANES), 0)
    lane = lax.broadcasted_iota(jnp.int32, (8, LANES), 1)
    m = jnp.where(lane // (LANES // (2 * STEP)) == row, m, 0.0)
    return jnp.sum(m, axis=0, keepdims=True)


def hops_kernel(j, local, send, hops, own, low, high, before, lx, ly, lz, lzb, lt, ltb, *rest):
    links = (lx, ly, lz, lzb, lt, ltb)
    out, moments, v0, v1, v2 = rest
    for k in range(6):
        for x in range(2):
            v0[k, x] = low[k, x]
            v0[k, 2 + x] = own[k, x]
            v0[k, 4 + x] = high[k, x]
    m = before[...] if before is not None else None
    if j == 1:
        m = norm_row(v0, 2, jnp.zeros((8, LANES), F32), 0)
    if hops == 1:
        hop(v0.at[:, 1:5], v2, 2, 1, links)
        m = norm_row(v2, 0, m, j)
    else:
        dst = v2 if local else out
        hop(v0, v1, 4, 0, links)
        hop(v1, dst, 2, 1, links)
        m = norm_row(v1, 1, m, j)
        if j + 1 < 2 * STEP:
            m = norm_row(dst, 0, m, j + 1)
    if local:
        for k in range(6):
            for x in range(2):
                out[k, x] = v2[k, x, 4:8]
    moments[...] = message_row(m) if send else m


def field_rows(ref, k, x):
    if ref.ndim == 6:
        return ref[0, k // 3, k % 3, x]
    v = ref[k, x]
    return v if v.shape[0] == 4 else v[4:8]


def restart_kernel(mass, gathered, shifts, b, hb, h2b, h3b, h4b, out, state):
    one = jnp.ones((8, LANES), F32)
    m = jnp.full((8, LANES), mass[0], F32)
    m2 = Pair(m * m, jnp.zeros_like(one))
    s = first_state(summed_moments(gathered[...]), m2, shifts[...])
    leaves, _ = jax.tree_util.tree_flatten(s)
    for i, leaf in enumerate(leaves):
        state[i : i + 1] = leaf[0:1]
    rest, top = s["handover"]
    c = [rest[0], -rest[1], rest[2], -rest[3], top]
    c = [v[0:4] for v in c]
    for k in range(6):
        for x in range(2):
            t = c[0] * field_rows(b, k, x)
            for w, ref in zip(c[1:], (hb, h2b, h3b, h4b)):
                t = t + w * field_rows(ref, k, x)
            out[k, x] = t


def finish_kernel(tree, mass, gathered, shifts, residues, state, before, *refs):
    fields, out, act = refs[:8], refs[8], refs[9]
    one = jnp.ones((8, LANES), F32)
    m = jnp.full((8, LANES), mass[0], F32)
    m2 = Pair(m * m, jnp.zeros_like(one))
    leaves = [
        jnp.broadcast_to(state[i : i + 1], (8, LANES)) for i in range(tree.num_leaves)
    ]
    s = jax.tree_util.tree_unflatten(tree, leaves)
    s = run_steps(STEP, summed_moments(gathered[...]), s, m2, one, shifts[...], True)
    weights = residues[...]
    c = [
        jnp.broadcast_to(
            jnp.sum(weights * s["sol"][j], axis=1, keepdims=True), (8, LANES)
        )
        for j in range(2 * STEP)
    ]
    powers = summed_moments(before[...])
    t = c[0] * powers[0].h
    for j in range(1, STEP):
        t = t + c[j] * powers[j].h
    act[...] = t
    c = [(v if j % 2 == 0 else -v)[0:4] for j, v in enumerate(c)]
    for k in range(6):
        for x in range(2):
            t = c[0] * field_rows(fields[0], k, x)
            for w, ref in zip(c[1:], fields[1:]):
                t = t + w * field_rows(ref, k, x)
            out[0, k // 3, k % 3, x] = t


def both_ways(x_up, x_down, axis):
    n = lax.axis_size(axis)
    up = [(i, (i + 1) % n) for i in range(n)]
    return lax.ppermute(x_up, axis, up), lax.ppermute(x_down, axis, [(b, a) for a, b in up])


def everyone(row):
    n = lax.axis_size(ZT_XY)
    rows = lax.all_to_all(jnp.broadcast_to(row[None], (n, 1, LANES)), ZT_XY, 0, 0, tiled=True)
    rows = rows.reshape(n, LANES)
    return jnp.pad(rows, ((0, -n % 8), (0, 0)))


def field_scratch():
    return [pltpu.VMEM((6, n, ROWS, LANES), F32) for n in (6, 4, 2)]


def on_device(source, links, shifts, residues, mass):
    grp = lax.axis_index("grp")
    xs, ts = source.shape[3], source.shape[4]
    last = lax.axis_index(ZT) == lax.axis_size(ZT) - 1
    where = jnp.stack([grp, last.astype(jnp.int32)])
    lane_shifts = jnp.broadcast_to(
        jnp.pad(shifts, (0, LANES - shifts.shape[0]), constant_values=1.0), (8, LANES)
    )
    lane_residues = jnp.broadcast_to(
        jnp.pad(residues, (0, LANES - residues.shape[0])), (8, LANES)
    )
    other = lax.ppermute(links, "grp", [(0, 1), (1, 0)])
    small = (6, xs, ts, LANES)
    tall = (6, xs, ROWS, LANES)
    (mine,) = call(fold_kernel, "fold", [(78, xs, ts, LANES)], (where, links, other, source), 1)
    low, high = both_ways(mine, mine, ZT)
    wide, up, down = call(
        wide_links_kernel,
        "wide_links",
        [(78, xs, ROWS, LANES), (102, ROWS, LANES), (84, ROWS, LANES)],
        (mine, low, high),
    )
    low, high = both_ways(up, down, XY)
    shapes = [(18, LX_N, ROWS, LANES)] + [(18, L_N, ROWS, LANES)] * 5
    f2, m, *w = call(
        first_hops_kernel,
        "first_hops",
        [tall, (8, LANES), *shapes],
        (wide, low, high),
        scratch=field_scratch()[:2],
    )

    def hops(field, m, j, local, send=False, count=2):
        low, high = both_ways(field, field, XY)
        first = m is None
        body = functools.partial(hops_kernel, j, local, send, count)
        if first:
            plain = body

            def body(own, low, high, *rest):
                plain(own, low, high, None, *rest)

        args = (field, low, high) + (() if first else (m,)) + tuple(w)
        out, m = call(
            body,
            "hops",
            [small if local else tall, (1, LANES) if send else (8, LANES)],
            args,
            scratch=field_scratch(),
        )
        return out, m

    def taller(field):
        low, high = both_ways(field, field, ZT)
        return call(wide_field_kernel, "wide_field", [tall], (field, low, high))[0]

    f4, m = hops(f2, m, 3, True)
    f6, m = hops(taller(f4), m, 5, False)
    f8, m = hops(f6, m, 7, True, True)
    gathered = everyone(m)
    leaves, tree = state_shape()
    count = -(-len(leaves) // 8) * 8
    r0, state = call(
        restart_kernel,
        "restart",
        [small, (count, LANES)],
        (mass, gathered, lane_shifts, source, f2, f4, f6, f8),
        1,
    )
    r2, m = hops(taller(r0), None, 1, False)
    r4, m = hops(r2, m, 3, True)
    r6, m = hops(taller(r4), m, 5, False)
    _, m = hops(r6, m, 7, True, True, 1)
    rational, act = call(
        functools.partial(finish_kernel, tree),
        "finish",
        [source.shape, (8, LANES)],
        (mass, everyone(m), lane_shifts, lane_residues, state, gathered)
        + (source, f2, f4, f6, r0, r2, r4, r6),
        1,
    )
    act = act[0:1]
    total = act + lax.ppermute(act, "grp", [(0, 1), (1, 0)])
    sites = xs * lax.axis_size(XY) * ts * lax.axis_size(ZT) * LANES
    sites *= source.shape[0] * lax.axis_size("grp")
    return (rational, (total / sites)[0, 0:1])


def solution(mesh):
    if mesh.size == 512:
        shape = (mesh.shape["grp"], 4, 4, 8, 2)
    else:
        shape = (mesh.shape["grp"], mesh.shape["zt"], 1, mesh.shape["xy"], 1)
    torus = Mesh(mesh.devices.reshape(shape), ("grp", "zt_0", "zt_1", "xy_0", "xy_1"))
    placed = (
        P("grp", None, None, XY, ZT, None),
        P("grp", None, None, None, XY, ZT, None),
        P(),
        P(),
        P(),
    )
    return jax.shard_map(
        on_device,
        mesh=torus,
        in_specs=placed,
        out_specs=(P("grp", None, None, XY, ZT, None), P()),
        check_vma=False,
    )
```

time: 704 us -> 218 us (0.31)
  the two profiles are of different devices: /device:TPU:27 before, /device:TPU:2 now
where the time goes in v1:
time: 218 us; the launch traced here: 217 us
  starting transfers between devices  103 us (47%)
  waiting for transfers between devices  83.9 us (38%)
  Pallas kernels  20.4 us (9%)
  local copies, waits for them, and re-layouts  8.06 us (4%)
    ppermute x12, starting transfers between devices, both_ways(): lax.ppermute(x_down, axis, [(b, a) for a, b in up])  50.7 us
    all_to_all x2, starting transfers between devices, everyone(): lax.all_to_all(jnp.broadcast_to(row[None], (n, 1, LANES)), ZT_XY, 0, 0, t...  32.5 us
    all_to_all x2, waiting for transfers between devices, everyone(): lax.all_to_all(jnp.broadcast_to(row[None], (n, 1, LANES)), ZT_XY, 0, 0, t...  28.8 us
    ppermute x12, waiting for transfers between devices, both_ways(): lax.ppermute(x_up, axis, up)  27 us
    ppermute x12, waiting for transfers between devices, both_ways(): lax.ppermute(x_down, axis, [(b, a) for a, b in up])  21.5 us
    pallas_call x15, Pallas kernels, call(): pl.pallas_call(body, name=name, in_specs=specs, out_specs=vm(len(outs)),...  20.4 us
    ppermute x12, starting transfers between devices, both_ways(): lax.ppermute(x_up, axis, up)  13 us
    unnamed x36, local copies, waits for them, and re-layouts  6.59 us
  transfers between devices with their start and end apart: 28, of which 19 were waited for; matrix products, arithmetic and copies ran while one was open for 0% of the time, Pallas kernels for 0%

profile of v1, /device:TPU:2, one launch (start us, length us, event | category | flops | bytes accessed | tf_op | source)
XLA Modules:
  0.0 217.2 jit_solution(8088360625928837969)
XLA Ops:
  0.6 3.5 %collective-permute-start = (f32[2,2,3,3,2,4,128]{6,5,4,3,2,1,0:T(4,128)}, f32[2,2,3,3,2,4,128]{6,5,4,3,2,1,0:T(4,128)S(1)}, u32[]{:S(2)}, u32[]{:S(2)}) collective-permute-start(f32[2,2,3,3,2,4,128]{6,5,4,3,2,1,0:T(4,128)} %own.1), channel_id=1, source_target_pairs={{0,256},{256,0},{1,257},{257,1},{2,258},{258,2},{3,259},{259,3},{4... | collective-permute-start | bytes 442376 | tf_op jit(solution)/shard_map/ppermute | solution.py:594
  4.2 4.1 %collective-permute-done.other = f32[2,2,3,3,2,4,128]{6,5,4,3,2,1,0:T(4,128)S(1)} collective-permute-done((f32[2,2,3,3,2,4,128]{6,5,4,3,2,1,0:T(4,128)}, f32[2,2,3,3,2,4,128]{6,5,4,3,2,1,0:T(4,128)S(1)}, u32[]{:S(2)}, u32[]{:S(2)}) %collective-permute-start) | collective-permute-done | bytes 147488 | tf_op jit(solution)/shard_map/ppermute | solution.py:594
  10.6 4.5 %collective-permute-start.1 = (f32[78,2,4,128]{3,2,1,0:T(4,128)S(1)}, f32[78,2,4,128]{3,2,1,0:T(4,128)S(1)}, u32[]{:S(2)}, u32[]{:S(2)}) collective-permute-start(f32[78,2,4,128]{3,2,1,0:T(4,128)S(1)} %fold.1.own), channel_id=1, source_target_pairs={{0,16},{16,32},{32,48},{48,64},{64,80},{80,96},{96,112},{112,128},... | collective-permute-start | bytes 958472 | tf_op jit(solution)/shard_map/ppermute | solution.py:569
  15.1 4.4 %collective-permute-start.2 = (f32[78,2,4,128]{3,2,1,0:T(4,128)S(1)}, f32[78,2,4,128]{3,2,1,0:T(4,128)S(1)}, u32[]{:S(2)}, u32[]{:S(2)}) collective-permute-start(f32[78,2,4,128]{3,2,1,0:T(4,128)S(1)} %fold.1.own), channel_id=1, source_target_pairs={{16,0},{32,16},{48,32},{64,48},{80,64},{96,80},{112,96},{128,112},... | collective-permute-start | bytes 958472 | tf_op jit(solution)/shard_map/ppermute | solution.py:569
  19.5 8.5 %collective-permute-done.1.low = f32[78,2,4,128]{3,2,1,0:T(4,128)S(1)} collective-permute-done((f32[78,2,4,128]{3,2,1,0:T(4,128)S(1)}, f32[78,2,4,128]{3,2,1,0:T(4,128)S(1)}, u32[]{:S(2)}, u32[]{:S(2)}) %collective-permute-start.1) | collective-permute-done | bytes 319520 | tf_op jit(solution)/shard_map/ppermute | solution.py:569
  27.9 6.1 %collective-permute-done.2.high = f32[78,2,4,128]{3,2,1,0:T(4,128)S(1)} collective-permute-done((f32[78,2,4,128]{3,2,1,0:T(4,128)S(1)}, f32[78,2,4,128]{3,2,1,0:T(4,128)S(1)}, u32[]{:S(2)}, u32[]{:S(2)}) %collective-permute-start.2) | collective-permute-done | bytes 319520 | tf_op jit(solution)/shard_map/ppermute | solution.py:569
  35.2 8.6 %collective-permute-start.4 = (f32[84,16,128]{2,1,0:T(8,128)S(1)}, f32[84,16,128]{2,1,0:T(8,128)S(1)}, u32[]{:S(2)}, u32[]{:S(2)}) collective-permute-start(f32[84,16,128]{2,1,0:T(8,128)S(1)} %get-tuple-element.32), channel_id=1, source_target_pairs={{1,0},{2,1},{3,2},{4,3},{5,4},{6,5},{7,6},{8,7},{9,8},{10,9},{11,1... | collective-permute-start | bytes 2064392 | tf_op jit(solution)/shard_map/ppermute | solution.py:569
  43.8 8.5 %collective-permute-done.4.high = f32[84,16,128]{2,1,0:T(8,128)S(1)} collective-permute-done((f32[84,16,128]{2,1,0:T(8,128)S(1)}, f32[84,16,128]{2,1,0:T(8,128)S(1)}, u32[]{:S(2)}, u32[]{:S(2)}) %collective-permute-start.4) | collective-permute-done | bytes 688160 | tf_op jit(solution)/shard_map/ppermute | solution.py:569
  54.0 5.7 %first_hops.1 = (f32[6,2,16,128]{3,2,1,0:T(8,128)S(1)}, f32[8,128]{1,0:T(8,128)S(1)}, f32[18,5,16,128]{3,2,1,0:T(8,128)S(1)}, f32[18,4,16,128]{3,2,1,0:T(8,128)S...) custom-call(f32[78,2,16,128]{3,2,1,0:T(8,128)S(1)} %get-tuple-elemen, ...), custom_call_target="tpu_custom_call" | custom-call | tf_op jit(solution)/shard_map/first_hops/pallas_call | solution.py:287
  59.7 2.9 %collective-permute-start.6 = (f32[6,2,16,128]{3,2,1,0:T(8,128)S(1)}, f32[6,2,16,128]{3,2,1,0:T(8,128)S(1)}, u32[]{:S(2)}, u32[]{:S(2)}) collective-permute-start(f32[6,2,16,128]{3,2,1,0:T(8,128)S(1)} %get-tuple-element.33.own.hb.refs_1_), channel_id=1, source_target_pairs={{1,0},{2,1},{3,2},{4,3},{5,4},{6,5},{7,6},{8,7},{9,8},{10,9},{11,1... | collective-permute-start | bytes 294920 | tf_op jit(solution)/shard_map/ppermute | solution.py:569
  62.6 2.3 %collective-permute-done.5.low = f32[6,2,16,128]{3,2,1,0:T(8,128)S(1)} collective-permute-done((f32[6,2,16,128]{3,2,1,0:T(8,128)S(1)}, f32[6,2,16,128]{3,2,1,0:T(8,128)S(1)}, u32[]{:S(2)}, u32[]{:S(2)}) %collective-permute-start.5) | collective-permute-done | bytes 98336 | tf_op jit(solution)/shard_map/ppermute | solution.py:569
  66.2 4.0 %collective-permute-start.7 = (f32[6,2,4,128]{3,2,1,0:T(4,128)S(1)}, f32[6,2,4,128]{3,2,1,0:T(4,128)S(1)}, u32[]{:S(2)}, u32[]{:S(2)}) collective-permute-start(f32[6,2,4,128]{3,2,1,0:T(4,128)S(1)} %get-tuple-element.41.own.h2b.refs_2_), channel_id=1, source_target_pairs={{0,16},{16,32},{32,48},{48,64},{64,80},{80,96},{96,112},{112,128},... | collective-permute-start | bytes 73736 | tf_op jit(solution)/shard_map/ppermute | solution.py:569
  70.2 4.9 %collective-permute-start.8 = (f32[6,2,4,128]{3,2,1,0:T(4,128)S(1)}, f32[6,2,4,128]{3,2,1,0:T(4,128)S(1)}, u32[]{:S(2)}, u32[]{:S(2)}) collective-permute-start(f32[6,2,4,128]{3,2,1,0:T(4,128)S(1)} %get-tuple-element.41.own.h2b.refs_2_), channel_id=1, source_target_pairs={{16,0},{32,16},{48,32},{64,48},{80,64},{96,80},{112,96},{128,112},... | collective-permute-start | bytes 73736 | tf_op jit(solution)/shard_map/ppermute | solution.py:569
  80.7 3.0 %collective-permute-done.9.low = f32[6,2,16,128]{3,2,1,0:T(8,128)S(1)} collective-permute-done((f32[6,2,16,128]{3,2,1,0:T(8,128)S(1)}, f32[6,2,16,128]{3,2,1,0:T(8,128)S(1)}, u32[]{:S(2)}, u32[]{:S(2)}) %collective-permute-start.9) | collective-permute-done | bytes 98336 | tf_op jit(solution)/shard_map/ppermute | solution.py:569
  85.0 2.9 %collective-permute-start.12 = (f32[6,2,16,128]{3,2,1,0:T(8,128)S(1)}, f32[6,2,16,128]{3,2,1,0:T(8,128)S(1)}, u32[]{:S(2)}, u32[]{:S(2)}) collective-permute-start(f32[6,2,16,128]{3,2,1,0:T(8,128)S(1)} %get-tuple-element.43.own.h3b.refs_3_), channel_id=1, source_target_pairs={{1,0},{2,1},{3,2},{4,3},{5,4},{6,5},{7,6},{8,7},{9,8},{10,9},{11,1... | collective-permute-start | bytes 294920 | tf_op jit(solution)/shard_map/ppermute | solution.py:569
  87.9 2.3 %collective-permute-done.11.low = f32[6,2,16,128]{3,2,1,0:T(8,128)S(1)} collective-permute-done((f32[6,2,16,128]{3,2,1,0:T(8,128)S(1)}, f32[6,2,16,128]{3,2,1,0:T(8,128)S(1)}, u32[]{:S(2)}, u32[]{:S(2)}) %collective-permute-start.11) | collective-permute-done | bytes 98336 | tf_op jit(solution)/shard_map/ppermute | solution.py:569
  92.5 15.6 %all-to-all-start = ((f32[256,1,128]{2,1,0:T(1,128)}), f32[256,1,128]{2,1,0:T(1,128)S(1)}, u32[]{:S(2)}, u32[]{:S(2)}) async-start(f32[256,1,128]{2,1,0:T(1,128)} %broadcast_in_dim.23), calls=%async_computation | async-start | bytes 262144 | tf_op jit(solution)/shard_map/all_to_all | solution.py:574
  108.8 14.1 %all-to-all-done = f32[256,1,128]{2,1,0:T(1,128)S(1)} async-done(((f32[256,1,128]{2,1,0:T(1,128)}), f32[256,1,128]{2,1,0:T(1,128)S(1)}, u32[]{:S(2)}, u32[]{:S(2)}) %all-to-all-start) | async-done | bytes 131104 | tf_op jit(solution)/shard_map/all_to_all | solution.py:574
  126.6 6.7 %collective-permute-start.14 = (f32[6,2,4,128]{3,2,1,0:T(4,128)S(1)}, f32[6,2,4,128]{3,2,1,0:T(4,128)S(1)}, u32[]{:S(2)}, u32[]{:S(2)}) collective-permute-start(f32[6,2,4,128]{3,2,1,0:T(4,128)S(1)} %get-tuple-element.47.own.refs_4_), channel_id=1, source_target_pairs={{16,0},{32,16},{48,32},{64,48},{80,64},{96,80},{112,96},{128,112},... | collective-permute-start | bytes 73736 | tf_op jit(solution)/shard_map/ppermute | solution.py:569
  134.8 2.9 %collective-permute-start.16 = (f32[6,2,16,128]{3,2,1,0:T(8,128)S(1)}, f32[6,2,16,128]{3,2,1,0:T(8,128)S(1)}, u32[]{:S(2)}, u32[]{:S(2)}) collective-permute-start(f32[6,2,16,128]{3,2,1,0:T(8,128)S(1)} %wide_field.4.own), channel_id=1, source_target_pairs={{1,0},{2,1},{3,2},{4,3},{5,4},{6,5},{7,6},{8,7},{9,8},{10,9},{11,1... | collective-permute-start | bytes 294920 | tf_op jit(solution)/shard_map/ppermute | solution.py:569
  137.8 2.3 %collective-permute-done.15.low = f32[6,2,16,128]{3,2,1,0:T(8,128)S(1)} collective-permute-done((f32[6,2,16,128]{3,2,1,0:T(8,128)S(1)}, f32[6,2,16,128]{3,2,1,0:T(8,128)S(1)}, u32[]{:S(2)}, u32[]{:S(2)}) %collective-permute-start.15) | collective-permute-done | bytes 98336 | tf_op jit(solution)/shard_map/ppermute | solution.py:569
  142.5 3.0 %collective-permute-start.18 = (f32[6,2,16,128]{3,2,1,0:T(8,128)S(1)}, f32[6,2,16,128]{3,2,1,0:T(8,128)S(1)}, u32[]{:S(2)}, u32[]{:S(2)}) collective-permute-start(f32[6,2,16,128]{3,2,1,0:T(8,128)S(1)} %get-tuple-element.48.own.refs_5_), channel_id=1, source_target_pairs={{1,0},{2,1},{3,2},{4,3},{5,4},{6,5},{7,6},{8,7},{9,8},{10,9},{11,1... | collective-permute-start | bytes 294920 | tf_op jit(solution)/shard_map/ppermute | solution.py:569
  145.4 2.3 %collective-permute-done.17.low = f32[6,2,16,128]{3,2,1,0:T(8,128)S(1)} collective-permute-done((f32[6,2,16,128]{3,2,1,0:T(8,128)S(1)}, f32[6,2,16,128]{3,2,1,0:T(8,128)S(1)}, u32[]{:S(2)}, u32[]{:S(2)}) %collective-permute-start.17) | collective-permute-done | bytes 98336 | tf_op jit(solution)/shard_map/ppermute | solution.py:569
  151.3 6.9 %collective-permute-start.20 = (f32[6,2,4,128]{3,2,1,0:T(4,128)S(1)}, f32[6,2,4,128]{3,2,1,0:T(4,128)S(1)}, u32[]{:S(2)}, u32[]{:S(2)}) collective-permute-start(f32[6,2,4,128]{3,2,1,0:T(4,128)S(1)} %get-tuple-element.50.own.refs_6_), channel_id=1, source_target_pairs={{16,0},{32,16},{48,32},{64,48},{80,64},{96,80},{112,96},{128,112},... | collective-permute-start | bytes 73736 | tf_op jit(solution)/shard_map/ppermute | solution.py:569
  159.7 2.9 %collective-permute-start.22 = (f32[6,2,16,128]{3,2,1,0:T(8,128)S(1)}, f32[6,2,16,128]{3,2,1,0:T(8,128)S(1)}, u32[]{:S(2)}, u32[]{:S(2)}) collective-permute-start(f32[6,2,16,128]{3,2,1,0:T(8,128)S(1)} %wide_field.5.own), channel_id=1, source_target_pairs={{1,0},{2,1},{3,2},{4,3},{5,4},{6,5},{7,6},{8,7},{9,8},{10,9},{11,1... | collective-permute-start | bytes 294920 | tf_op jit(solution)/shard_map/ppermute | solution.py:569
  162.7 2.3 %collective-permute-done.21.low = f32[6,2,16,128]{3,2,1,0:T(8,128)S(1)} collective-permute-done((f32[6,2,16,128]{3,2,1,0:T(8,128)S(1)}, f32[6,2,16,128]{3,2,1,0:T(8,128)S(1)}, u32[]{:S(2)}, u32[]{:S(2)}) %collective-permute-start.21) | collective-permute-done | bytes 98336 | tf_op jit(solution)/shard_map/ppermute | solution.py:569
  166.3 3.0 %collective-permute-start.24 = (f32[6,2,16,128]{3,2,1,0:T(8,128)S(1)}, f32[6,2,16,128]{3,2,1,0:T(8,128)S(1)}, u32[]{:S(2)}, u32[]{:S(2)}) collective-permute-start(f32[6,2,16,128]{3,2,1,0:T(8,128)S(1)} %get-tuple-element.52.own.refs_7_), channel_id=1, source_target_pairs={{1,0},{2,1},{3,2},{4,3},{5,4},{6,5},{7,6},{8,7},{9,8},{10,9},{11,1... | collective-permute-start | bytes 294920 | tf_op jit(solution)/shard_map/ppermute | solution.py:569
  173.3 16.8 %all-to-all-start.1 = ((f32[256,1,128]{2,1,0:T(1,128)}), f32[256,1,128]{2,1,0:T(1,128)S(1)}, u32[]{:S(2)}, u32[]{:S(2)}) async-start(f32[256,1,128]{2,1,0:T(1,128)} %broadcast_in_dim.26), calls=%async_computation.1 | async-start | bytes 262144 | tf_op jit(solution)/shard_map/all_to_all | solution.py:574
  190.2 14.7 %all-to-all-done.1 = f32[256,1,128]{2,1,0:T(1,128)S(1)} async-done(((f32[256,1,128]{2,1,0:T(1,128)}), f32[256,1,128]{2,1,0:T(1,128)S(1)}, u32[]{:S(2)}, u32[]{:S(2)}) %all-to-all-start.1) | async-done | bytes 131104 | tf_op jit(solution)/shard_map/all_to_all | solution.py:574
  208.7 2.5 %finish.1 = (f32[1,2,3,2,4,128]{5,4,3,2,1,0:T(4,128)}, f32[8,128]{1,0:T(8,128)S(1)}) custom-call(f32[1]{0:T(128)S(6)} %copy.7.mass, f32[256,128]{1,0:T(8,128)S(1)} %bitcast.10, f32[8,128]{1,0:T(8,128)S(1)} %broadcast_in_dim.24.shifts, f32[8,128]{1,0:T(8,128)S(1)} %broadcast_in_dim.27.residues, f32[48,128]{1,0:T(8,128)S(1)} %copy-done.15, ...), custom_call_target="tpu_custom_call" | custom-call | tf_op jit(solution)/shard_map/finish/pallas_call | solution.py:287
  211.2 2.9 %collective-permute-start.25 = (f32[1,128]{1,0:T(1,128)S(1)}, f32[1,128]{1,0:T(1,128)S(1)}, u32[]{:S(2)}, u32[]{:S(2)}) collective-permute-start(f32[1,128]{1,0:T(1,128)S(1)} %slice.6), channel_id=1, source_target_pairs={{0,256},{256,0},{1,257},{257,1},{2,258},{258,2},{3,259},{259,3},{4... | collective-permute-start | bytes 1544 | tf_op jit(solution)/shard_map/ppermute | solution.py:665
  214.1 2.5 %collective-permute-done.25 = f32[1,128]{1,0:T(1,128)S(1)} collective-permute-done((f32[1,128]{1,0:T(1,128)S(1)}, f32[1,128]{1,0:T(1,128)S(1)}, u32[]{:S(2)}, u32[]{:S(2)}) %collective-permute-start.25) | collective-permute-done | bytes 544 | tf_op jit(solution)/shard_map/ppermute | solution.py:665
  (84 shorter events, 37.9 us)
Async XLA Ops:
  0.6 7.7 %collective-permute-start = (f32[2,2,3,3,2,4,128]{6,5,4,3,2,1,0:T(4,128)}, f32[2,2,3,3,2,4,128]{6,5,4,3,2,1,0:T(4,128)S(1)}, u32[]{:S(2)}, u32[]{:S(2)}) collective-permute-start(f32[2,2,3,3,2,4,128]{6,5,4,3,2,1,0:T(4,128)} %own.1), channel_id=1, source_target_pairs={{0,256},{256,0},{1,257},{257,1},{2,258},{258,2},{3,259},{259,3},{4... | collective-permute-start | bytes 442376 | tf_op jit(solution)/shard_map/ppermute | solution.py:594
  10.6 17.3 %collective-permute-start.1 = (f32[78,2,4,128]{3,2,1,0:T(4,128)S(1)}, f32[78,2,4,128]{3,2,1,0:T(4,128)S(1)}, u32[]{:S(2)}, u32[]{:S(2)}) collective-permute-start(f32[78,2,4,128]{3,2,1,0:T(4,128)S(1)} %fold.1.own), channel_id=1, source_target_pairs={{0,16},{16,32},{32,48},{48,64},{64,80},{80,96},{96,112},{112,128},... | collective-permute-start | bytes 958472 | tf_op jit(solution)/shard_map/ppermute | solution.py:569
  15.1 18.9 %collective-permute-start.2 = (f32[78,2,4,128]{3,2,1,0:T(4,128)S(1)}, f32[78,2,4,128]{3,2,1,0:T(4,128)S(1)}, u32[]{:S(2)}, u32[]{:S(2)}) collective-permute-start(f32[78,2,4,128]{3,2,1,0:T(4,128)S(1)} %fold.1.own), channel_id=1, source_target_pairs={{16,0},{32,16},{48,32},{64,48},{80,64},{96,80},{112,96},{128,112},... | collective-permute-start | bytes 958472 | tf_op jit(solution)/shard_map/ppermute | solution.py:569
  35.2 18.8 %collective-permute-start.3 = (f32[102,16,128]{2,1,0:T(8,128)S(1)}, f32[102,16,128]{2,1,0:T(8,128)S(1)}, u32[]{:S(2)}, u32[]{:S(2)}) collective-permute-start(f32[102,16,128]{2,1,0:T(8,128)S(1)} %get-tuple-element.31), channel_id=1, source_target_pairs={{0,1},{1,2},{2,3},{3,4},{4,5},{5,6},{6,7},{7,8},{8,9},{9,10},{10,1... | collective-permute-start | bytes 2506760 | tf_op jit(solution)/shard_map/ppermute | solution.py:569
  35.2 17.0 %collective-permute-start.4 = (f32[84,16,128]{2,1,0:T(8,128)S(1)}, f32[84,16,128]{2,1,0:T(8,128)S(1)}, u32[]{:S(2)}, u32[]{:S(2)}) collective-permute-start(f32[84,16,128]{2,1,0:T(8,128)S(1)} %get-tuple-element.32), channel_id=1, source_target_pairs={{1,0},{2,1},{3,2},{4,3},{5,4},{6,5},{7,6},{8,7},{9,8},{10,9},{11,1... | collective-permute-start | bytes 2064392 | tf_op jit(solution)/shard_map/ppermute | solution.py:569
  59.7 30.6 %copy-start = (f32[18,4,16,128]{3,2,1,0:T(8,128)}, f32[18,4,16,128]{3,2,1,0:T(8,128)S(1)}, u32[]{:S(2)}) copy-start(f32[18,4,16,128]{3,2,1,0:T(8,128)S(1)} %get-tuple-element.40.ltb.rest_5_) | copy-start | bytes 1769476
  59.7 5.3 %collective-permute-start.5 = (f32[6,2,16,128]{3,2,1,0:T(8,128)S(1)}, f32[6,2,16,128]{3,2,1,0:T(8,128)S(1)}, u32[]{:S(2)}, u32[]{:S(2)}) collective-permute-start(f32[6,2,16,128]{3,2,1,0:T(8,128)S(1)} %get-tuple-element.33.own.hb.refs_1_), channel_id=1, source_target_pairs={{0,1},{1,2},{2,3},{3,4},{4,5},{5,6},{6,7},{7,8},{8,9},{9,10},{10,1... | collective-permute-start | bytes 294920 | tf_op jit(solution)/shard_map/ppermute | solution.py:569
  59.7 5.2 %collective-permute-start.6 = (f32[6,2,16,128]{3,2,1,0:T(8,128)S(1)}, f32[6,2,16,128]{3,2,1,0:T(8,128)S(1)}, u32[]{:S(2)}, u32[]{:S(2)}) collective-permute-start(f32[6,2,16,128]{3,2,1,0:T(8,128)S(1)} %get-tuple-element.33.own.hb.refs_1_), channel_id=1, source_target_pairs={{1,0},{2,1},{3,2},{4,3},{5,4},{6,5},{7,6},{8,7},{9,8},{10,9},{11,1... | collective-permute-start | bytes 294920 | tf_op jit(solution)/shard_map/ppermute | solution.py:569
  66.2 56.7 %copy-start.7 = (f32[6,2,4,128]{3,2,1,0:T(4,128)}, f32[6,2,4,128]{3,2,1,0:T(4,128)S(1)}, u32[]{:S(2)}) copy-start(f32[6,2,4,128]{3,2,1,0:T(4,128)S(1)} %get-tuple-element.41.own.h2b.refs_2_) | copy-start | bytes 73732
  66.2 8.9 %collective-permute-start.7 = (f32[6,2,4,128]{3,2,1,0:T(4,128)S(1)}, f32[6,2,4,128]{3,2,1,0:T(4,128)S(1)}, u32[]{:S(2)}, u32[]{:S(2)}) collective-permute-start(f32[6,2,4,128]{3,2,1,0:T(4,128)S(1)} %get-tuple-element.41.own.h2b.refs_2_), channel_id=1, source_target_pairs={{0,16},{16,32},{32,48},{48,64},{64,80},{80,96},{96,112},{112,128},... | collective-permute-start | bytes 73736 | tf_op jit(solution)/shard_map/ppermute | solution.py:569
  70.2 6.6 %collective-permute-start.8 = (f32[6,2,4,128]{3,2,1,0:T(4,128)S(1)}, f32[6,2,4,128]{3,2,1,0:T(4,128)S(1)}, u32[]{:S(2)}, u32[]{:S(2)}) collective-permute-start(f32[6,2,4,128]{3,2,1,0:T(4,128)S(1)} %get-tuple-element.41.own.h2b.refs_2_), channel_id=1, source_target_pairs={{16,0},{32,16},{48,32},{64,48},{80,64},{96,80},{112,96},{128,112},... | collective-permute-start | bytes 73736 | tf_op jit(solution)/shard_map/ppermute | solution.py:569
  76.9 3.8 %collective-permute-start.10 = (f32[6,2,16,128]{3,2,1,0:T(8,128)S(1)}, f32[6,2,16,128]{3,2,1,0:T(8,128)S(1)}, u32[]{:S(2)}, u32[]{:S(2)}) collective-permute-start(f32[6,2,16,128]{3,2,1,0:T(8,128)S(1)} %wide_field.3.own), channel_id=1, source_target_pairs={{1,0},{2,1},{3,2},{4,3},{5,4},{6,5},{7,6},{8,7},{9,8},{10,9},{11,1... | collective-permute-start | bytes 294920 | tf_op jit(solution)/shard_map/ppermute | solution.py:569
  78.4 5.3 %collective-permute-start.9 = (f32[6,2,16,128]{3,2,1,0:T(8,128)S(1)}, f32[6,2,16,128]{3,2,1,0:T(8,128)S(1)}, u32[]{:S(2)}, u32[]{:S(2)}) collective-permute-start(f32[6,2,16,128]{3,2,1,0:T(8,128)S(1)} %wide_field.3.own), channel_id=1, source_target_pairs={{0,1},{1,2},{2,3},{3,4},{4,5},{5,6},{6,7},{7,8},{8,9},{9,10},{10,1... | collective-permute-start | bytes 294920 | tf_op jit(solution)/shard_map/ppermute | solution.py:569
  85.0 5.3 %collective-permute-start.11 = (f32[6,2,16,128]{3,2,1,0:T(8,128)S(1)}, f32[6,2,16,128]{3,2,1,0:T(8,128)S(1)}, u32[]{:S(2)}, u32[]{:S(2)}) collective-permute-start(f32[6,2,16,128]{3,2,1,0:T(8,128)S(1)} %get-tuple-element.43.own.h3b.refs_3_), channel_id=1, source_target_pairs={{0,1},{1,2},{2,3},{3,4},{4,5},{5,6},{6,7},{7,8},{8,9},{9,10},{10,1... | collective-permute-start | bytes 294920 | tf_op jit(solution)/shard_map/ppermute | solution.py:569
  85.0 5.2 %collective-permute-start.12 = (f32[6,2,16,128]{3,2,1,0:T(8,128)S(1)}, f32[6,2,16,128]{3,2,1,0:T(8,128)S(1)}, u32[]{:S(2)}, u32[]{:S(2)}) collective-permute-start(f32[6,2,16,128]{3,2,1,0:T(8,128)S(1)} %get-tuple-element.43.own.h3b.refs_3_), channel_id=1, source_target_pairs={{1,0},{2,1},{3,2},{4,3},{5,4},{6,5},{7,6},{8,7},{9,8},{10,9},{11,1... | collective-permute-start | bytes 294920 | tf_op jit(solution)/shard_map/ppermute | solution.py:569
  90.2 32.6 %copy-start.6 = (f32[1,2,3,2,4,128]{5,4,3,2,1,0:T(4,128)S(1)}, f32[1,2,3,2,4,128]{5,4,3,2,1,0:T(4,128)}, u32[]{:S(2)}) copy-start(f32[1,2,3,2,4,128]{5,4,3,2,1,0:T(4,128)} %refs_0_.1) | copy-start | bytes 73732
  92.5 30.4 %all-to-all-start = ((f32[256,1,128]{2,1,0:T(1,128)}), f32[256,1,128]{2,1,0:T(1,128)S(1)}, u32[]{:S(2)}, u32[]{:S(2)}) async-start(f32[256,1,128]{2,1,0:T(1,128)} %broadcast_in_dim.23), calls=%async_computation | async-start | bytes 262144 | tf_op jit(solution)/shard_map/all_to_all | solution.py:574
  124.4 8.9 %collective-permute-start.13 = (f32[6,2,4,128]{3,2,1,0:T(4,128)S(1)}, f32[6,2,4,128]{3,2,1,0:T(4,128)S(1)}, u32[]{:S(2)}, u32[]{:S(2)}) collective-permute-start(f32[6,2,4,128]{3,2,1,0:T(4,128)S(1)} %get-tuple-element.47.own.refs_4_), channel_id=1, source_target_pairs={{0,16},{16,32},{32,48},{48,64},{64,80},{80,96},{96,112},{112,128},... | collective-permute-start | bytes 73736 | tf_op jit(solution)/shard_map/ppermute | solution.py:569
  126.6 8.2 %collective-permute-start.14 = (f32[6,2,4,128]{3,2,1,0:T(4,128)S(1)}, f32[6,2,4,128]{3,2,1,0:T(4,128)S(1)}, u32[]{:S(2)}, u32[]{:S(2)}) collective-permute-start(f32[6,2,4,128]{3,2,1,0:T(4,128)S(1)} %get-tuple-element.47.own.refs_4_), channel_id=1, source_target_pairs={{16,0},{32,16},{48,32},{64,48},{80,64},{96,80},{112,96},{128,112},... | collective-permute-start | bytes 73736 | tf_op jit(solution)/shard_map/ppermute | solution.py:569
  134.8 5.3 %collective-permute-start.15 = (f32[6,2,16,128]{3,2,1,0:T(8,128)S(1)}, f32[6,2,16,128]{3,2,1,0:T(8,128)S(1)}, u32[]{:S(2)}, u32[]{:S(2)}) collective-permute-start(f32[6,2,16,128]{3,2,1,0:T(8,128)S(1)} %wide_field.4.own), channel_id=1, source_target_pairs={{0,1},{1,2},{2,3},{3,4},{4,5},{5,6},{6,7},{7,8},{8,9},{9,10},{10,1... | collective-permute-start | bytes 294920 | tf_op jit(solution)/shard_map/ppermute | solution.py:569
  134.8 5.2 %collective-permute-start.16 = (f32[6,2,16,128]{3,2,1,0:T(8,128)S(1)}, f32[6,2,16,128]{3,2,1,0:T(8,128)S(1)}, u32[]{:S(2)}, u32[]{:S(2)}) collective-permute-start(f32[6,2,16,128]{3,2,1,0:T(8,128)S(1)} %wide_field.4.own), channel_id=1, source_target_pairs={{1,0},{2,1},{3,2},{4,3},{5,4},{6,5},{7,6},{8,7},{9,8},{10,9},{11,1... | collective-permute-start | bytes 294920 | tf_op jit(solution)/shard_map/ppermute | solution.py:569
  142.5 5.3 %collective-permute-start.17 = (f32[6,2,16,128]{3,2,1,0:T(8,128)S(1)}, f32[6,2,16,128]{3,2,1,0:T(8,128)S(1)}, u32[]{:S(2)}, u32[]{:S(2)}) collective-permute-start(f32[6,2,16,128]{3,2,1,0:T(8,128)S(1)} %get-tuple-element.48.own.refs_5_), channel_id=1, source_target_pairs={{0,1},{1,2},{2,3},{3,4},{4,5},{5,6},{6,7},{7,8},{8,9},{9,10},{10,1... | collective-permute-start | bytes 294920 | tf_op jit(solution)/shard_map/ppermute | solution.py:569
  142.5 5.2 %collective-permute-start.18 = (f32[6,2,16,128]{3,2,1,0:T(8,128)S(1)}, f32[6,2,16,128]{3,2,1,0:T(8,128)S(1)}, u32[]{:S(2)}, u32[]{:S(2)}) collective-permute-start(f32[6,2,16,128]{3,2,1,0:T(8,128)S(1)} %get-tuple-element.48.own.refs_5_), channel_id=1, source_target_pairs={{1,0},{2,1},{3,2},{4,3},{5,4},{6,5},{7,6},{8,7},{9,8},{10,9},{11,1... | collective-permute-start | bytes 294920 | tf_op jit(solution)/shard_map/ppermute | solution.py:569
  149.0 9.2 %collective-permute-start.19 = (f32[6,2,4,128]{3,2,1,0:T(4,128)S(1)}, f32[6,2,4,128]{3,2,1,0:T(4,128)S(1)}, u32[]{:S(2)}, u32[]{:S(2)}) collective-permute-start(f32[6,2,4,128]{3,2,1,0:T(4,128)S(1)} %get-tuple-element.50.own.refs_6_), channel_id=1, source_target_pairs={{0,16},{16,32},{32,48},{48,64},{64,80},{80,96},{96,112},{112,128},... | collective-permute-start | bytes 73736 | tf_op jit(solution)/shard_map/ppermute | solution.py:569
  151.3 8.4 %collective-permute-start.20 = (f32[6,2,4,128]{3,2,1,0:T(4,128)S(1)}, f32[6,2,4,128]{3,2,1,0:T(4,128)S(1)}, u32[]{:S(2)}, u32[]{:S(2)}) collective-permute-start(f32[6,2,4,128]{3,2,1,0:T(4,128)S(1)} %get-tuple-element.50.own.refs_6_), channel_id=1, source_target_pairs={{16,0},{32,16},{48,32},{64,48},{80,64},{96,80},{112,96},{128,112},... | collective-permute-start | bytes 73736 | tf_op jit(solution)/shard_map/ppermute | solution.py:569
  159.7 5.3 %collective-permute-start.21 = (f32[6,2,16,128]{3,2,1,0:T(8,128)S(1)}, f32[6,2,16,128]{3,2,1,0:T(8,128)S(1)}, u32[]{:S(2)}, u32[]{:S(2)}) collective-permute-start(f32[6,2,16,128]{3,2,1,0:T(8,128)S(1)} %wide_field.5.own), channel_id=1, source_target_pairs={{0,1},{1,2},{2,3},{3,4},{4,5},{5,6},{6,7},{7,8},{8,9},{9,10},{10,1... | collective-permute-start | bytes 294920 | tf_op jit(solution)/shard_map/ppermute | solution.py:569
  159.7 5.2 %collective-permute-start.22 = (f32[6,2,16,128]{3,2,1,0:T(8,128)S(1)}, f32[6,2,16,128]{3,2,1,0:T(8,128)S(1)}, u32[]{:S(2)}, u32[]{:S(2)}) collective-permute-start(f32[6,2,16,128]{3,2,1,0:T(8,128)S(1)} %wide_field.5.own), channel_id=1, source_target_pairs={{1,0},{2,1},{3,2},{4,3},{5,4},{6,5},{7,6},{8,7},{9,8},{10,9},{11,1... | collective-permute-start | bytes 294920 | tf_op jit(solution)/shard_map/ppermute | solution.py:569
  166.3 5.3 %collective-permute-start.23 = (f32[6,2,16,128]{3,2,1,0:T(8,128)S(1)}, f32[6,2,16,128]{3,2,1,0:T(8,128)S(1)}, u32[]{:S(2)}, u32[]{:S(2)}) collective-permute-start(f32[6,2,16,128]{3,2,1,0:T(8,128)S(1)} %get-tuple-element.52.own.refs_7_), channel_id=1, source_target_pairs={{0,1},{1,2},{2,3},{3,4},{4,5},{5,6},{6,7},{7,8},{8,9},{9,10},{10,1... | collective-permute-start | bytes 294920 | tf_op jit(solution)/shard_map/ppermute | solution.py:569
  166.3 5.2 %collective-permute-start.24 = (f32[6,2,16,128]{3,2,1,0:T(8,128)S(1)}, f32[6,2,16,128]{3,2,1,0:T(8,128)S(1)}, u32[]{:S(2)}, u32[]{:S(2)}) collective-permute-start(f32[6,2,16,128]{3,2,1,0:T(8,128)S(1)} %get-tuple-element.52.own.refs_7_), channel_id=1, source_target_pairs={{1,0},{2,1},{3,2},{4,3},{5,4},{6,5},{7,6},{8,7},{9,8},{10,9},{11,1... | collective-permute-start | bytes 294920 | tf_op jit(solution)/shard_map/ppermute | solution.py:569
  171.5 18.6 %copy-start.17 = (f32[12]{0:T(128)S(1)}, f32[12]{0:T(128)}, u32[]{:S(2)}) copy-start(f32[12]{0:T(128)} %param.8) | copy-start | bytes 148
  173.3 31.6 %all-to-all-start.1 = ((f32[256,1,128]{2,1,0:T(1,128)}), f32[256,1,128]{2,1,0:T(1,128)S(1)}, u32[]{:S(2)}, u32[]{:S(2)}) async-start(f32[256,1,128]{2,1,0:T(1,128)} %broadcast_in_dim.26), calls=%async_computation.1 | async-start | bytes 262144 | tf_op jit(solution)/shard_map/all_to_all | solution.py:574
  211.2 5.5 %collective-permute-start.25 = (f32[1,128]{1,0:T(1,128)S(1)}, f32[1,128]{1,0:T(1,128)S(1)}, u32[]{:S(2)}, u32[]{:S(2)}) collective-permute-start(f32[1,128]{1,0:T(1,128)S(1)} %slice.6), channel_id=1, source_target_pairs={{0,256},{256,0},{1,257},{257,1},{2,258},{258,2},{3,259},{259,3},{4... | collective-permute-start | bytes 1544 | tf_op jit(solution)/shard_map/ppermute | solution.py:665
  (14 other events, 97.2 us)

commit v2 on v1

v2 whole, which is shorter than its diff:
```python
import functools

import jax
import jax.numpy as jnp
from jax import lax
from jax.experimental import pallas as pl
from jax.experimental.pallas import tpu as pltpu
from jax.sharding import Mesh
from jax.sharding import PartitionSpec as P

NY = 2
NZ = 64
LANES = NY * NZ
STEP = 4
XY = ("xy_0", "xy_1")
ZT = ("zt_0", "zt_1")
ZT_XY = ("zt_0", "zt_1", "xy_0", "xy_1")
F32 = jnp.float32
ROWS = 16
REDUCE = ("zt_0", "zt_1", "xy_0")
LOCAL = (6, 8, LANES)


def two_sum(a, b):
    s = a + b
    t = s - a
    return s, (a - (s - t)) + (b - t)


def quick_sum(a, b):
    s = a + b
    return s, b - (s - a)


def halves(a):
    t = a * 4097.0
    h = t - (t - a)
    return h, a - h


def two_prod(a, b):
    p = a * b
    ah, al = halves(a)
    bh, bl = halves(b)
    return p, ((ah * bh - p) + ah * bl + al * bh) + al * bl


@jax.tree_util.register_pytree_node_class
class Pair:
    def __init__(self, h, l):
        self.h = h
        self.l = l

    def tree_flatten(self):
        return (self.h, self.l), None

    @classmethod
    def tree_unflatten(cls, _, leaves):
        return cls(*leaves)

    def __add__(self, o):
        a, e = two_sum(self.h, o.h)
        t, f = two_sum(self.l, o.l)
        a, e = quick_sum(a, e + t)
        return Pair(*quick_sum(a, e + f))

    def __neg__(self):
        return Pair(-self.h, -self.l)

    def __sub__(self, o):
        return self + (-o)

    def __mul__(self, o):
        p, e = two_prod(self.h, o.h)
        return Pair(*quick_sum(p, e + (self.h * o.l + self.l * o.h)))

    def times(self, f):
        p, e = two_prod(self.h, f)
        return Pair(*quick_sum(p, e + self.l * f))

    def __truediv__(self, o):
        q1 = self.h / o.h
        r = self - o.times(q1)
        q2 = r.h / o.h
        r = r - o.times(q2)
        a, b = quick_sum(q1, q2)
        return Pair(*quick_sum(a, b + r.h / o.h))


def plus(a, b):
    return b if a is None else a + b


def run_steps(first, moments, state, m2, one, shifts, final):
    size = STEP
    al, be, c, gam = (dict(state[n]) for n in ("al", "be", "c", "gam"))
    coef = dict(state["coef"])
    part, sol = dict(state["part"]), dict(state["sol"])
    zeta, zeta_old, zeta_new = state["zeta"], state["zeta_old"], state["zeta_new"]
    unit = Pair(one, jnp.zeros_like(one))
    table = {first: list(moments)}
    raised = {}
    if first:
        inv, own, low = {}, {}, {}
        for k in range(first):
            inv[k] = unit / al[k]
            own[k] = (unit + c[k] if k else unit) * inv[k] - m2
            if k:
                low[k] = c[k] * inv[k]
            table[k] = [None] * (2 * size)
        for i in range(1, 2 * size):
            for k in range(first - 1, -1, -1):
                if i < first - k:
                    continue
                t = None
                if table[k][i - 1] is not None:
                    t = plus(t, own[k] * table[k][i - 1])
                if table[k + 1][i - 1] is not None:
                    t = plus(t, -(inv[k] * table[k + 1][i - 1]))
                if k and table[k - 1][i - 1] is not None:
                    t = plus(t, -(low[k] * table[k - 1][i - 1]))
                table[k][i] = t
        rest, top = state["handover"]
        scale = one / top
        for k in range(first - 1):
            raised[k] = {k + 1: one}
        raised[first - 1] = {j: -(rest[j] * scale) for j in rest}
        raised[first - 1][first] = scale
    for i in range(size - 1):
        raised[first + i] = {first + i + 1: one}
    coef[first] = {first: one}
    lead, second = unit, None
    handover = None
    for d in range(size):
        k = first + d
        norm = lead * table[k][d]
        high = lead * table[k][d + 1]
        if second is not None:
            high = high + second * table[k][d]
        gam[k] = norm
        if k == 0:
            part = {0: jnp.ones_like(shifts)}
        else:
            ratio = norm / gam[k - 1]
            be[k - 1] = ratio
            step = zeta_new / zeta
            keep = ratio.h * step * step
            grown = {}
            for j in sorted(set(part) | set(coef[k])):
                t = None
                if j in coef[k]:
                    t = zeta_new * coef[k][j]
                if j in part:
                    t = plus(t, keep * part[j])
                grown[j] = t
            part = grown
            zeta_old, zeta = zeta, zeta_new
        curve = m2 * norm + high
        if k:
            curve = curve - ratio * norm / al[k - 1]
        a = norm / curve
        al[k] = a
        if k:
            a_old, b_old = al[k - 1].h, be[k - 1].h
            zeta_new = (
                zeta
                * zeta_old
                * a_old
                / (a.h * b_old * (zeta_old - zeta) + zeta_old * a_old * (1.0 + shifts * a.h))
            )
            c[k] = a * be[k - 1] / al[k - 1]
            keep_r = unit + c[k]
        else:
            zeta_new = zeta / (1.0 + shifts * a.h)
            keep_r = unit
        gain = a.h * zeta_new / zeta
        for j in part:
            sol[j] = plus(sol.get(j), gain * part[j])
        if d == size - 1 and final:
            break
        image = {}
        for j, v in coef[k].items():
            image[j] = plus(image.get(j), m2.h * v)
            if j == first + size - 1:
                continue
            for jj, w in raised[j].items():
                image[jj] = plus(image.get(jj), w * v)
        following = {}
        for j in sorted(set(coef[k]) | set(image) | set(coef.get(k - 1, {}))):
            t = None
            if j in coef[k]:
                t = keep_r.h * coef[k][j]
            if j in image:
                t = plus(t, -(a.h * image[j]))
            if k and j in coef[k - 1]:
                t = plus(t, -(c[k].h * coef[k - 1][j]))
            following[j] = t
        if d == size - 1:
            handover = (following, -(a.h * coef[k][first + size - 1]))
            break
        coef[k + 1] = following
        row = [None] * (2 * size)
        for i in range(2 * size - 1 - d):
            if table[k][i] is None or table[k][i + 1] is None:
                continue
            t = keep_r * table[k][i] - a * (m2 * table[k][i] + table[k][i + 1])
            if k and table[k - 1][i] is not None:
                t = t - c[k] * table[k - 1][i]
            row[i] = t
        table[k + 1] = row
        image_second = m2 * lead if second is None else m2 * lead + second
        lead, second = -(a * lead), keep_r * lead - a * image_second
    last = first + size - 1
    return {
        "al": al,
        "be": be,
        "c": c,
        "gam": {last: gam[last]},
        "coef": {last: coef[last]},
        "part": part,
        "sol": sol,
        "zeta": zeta,
        "zeta_old": zeta_old,
        "zeta_new": zeta_new,
        "handover": handover,
    }


def start_state(one):
    return {
        "al": {},
        "be": {},
        "c": {},
        "gam": {},
        "coef": {},
        "part": {},
        "sol": {},
        "zeta": one,
        "zeta_old": one,
        "zeta_new": one,
        "handover": None,
    }


def first_state(moments, m2, shifts):
    one = jnp.ones_like(shifts)
    return run_steps(0, moments, start_state(one), m2, one, shifts, False)


def summed_moments(gathered):
    rows = gathered.shape[0] // 8
    zero = jnp.zeros((8, LANES), F32)
    terms = [Pair(gathered[8 * i : 8 * i + 8], zero) for i in range(rows)]
    while len(terms) > 1:
        terms = [terms[i] + terms[i + 1] for i in range(0, len(terms) - 1, 2)] + (
            [terms[-1]] if len(terms) % 2 else []
        )
    t = terms[0]
    for s in (4, 2, 1):
        t = t + Pair(pltpu.roll(t.h, s, 0), pltpu.roll(t.l, s, 0))
    width = LANES // (2 * STEP)
    s = width // 2
    while s:
        t = t + Pair(pltpu.roll(t.h, LANES - s, 1), pltpu.roll(t.l, LANES - s, 1))
        s //= 2
    lane = lax.broadcasted_iota(jnp.int32, (8, LANES), 1)

    def spread(v, j):
        picked = jnp.where(lane == width * j, v, 0.0)
        return jnp.broadcast_to(jnp.sum(picked, axis=1, keepdims=True), (8, LANES))

    return [Pair(spread(t.h, j), spread(t.l, j)) for j in range(2 * STEP)]


def call(body, name, outs, args, smem=0, far=0, scratch=()):
    n = len(args)
    specs = [pl.BlockSpec(memory_space=pltpu.SMEM)] * smem
    specs += [pl.BlockSpec(memory_space=pltpu.VMEM)] * (n - smem - far)
    specs += [pl.BlockSpec(memory_space=pl.ANY)] * far
    return pl.pallas_call(
        body,
        name=name,
        in_specs=specs,
        out_specs=[pl.BlockSpec(memory_space=pltpu.VMEM)] * len(outs),
        out_shape=[jax.ShapeDtypeStruct(s, F32) for s in outs],
        scratch_shapes=list(scratch),
        compiler_params=pltpu.CompilerParams(vmem_limit_bytes=12 * 1024 * 1024),
    )(*args)


def wide_links_kernel(where, own, low, high, own_x, low_x, high_x, out, up, down):
    first = where[0] == 0
    flip = [jnp.where(where[i] == 1, -1.0, 1.0).astype(F32) for i in (1, 2, 3)]
    shape = (8, LANES)
    lane = lax.broadcasted_iota(jnp.int32, shape, 1)
    row = lax.broadcasted_iota(jnp.int32, shape, 0)
    x, t = row // 4, row % 4
    y = lane // NZ
    z = lane % NZ
    half = jnp.full(shape, 0.5, F32)
    etas = [
        half,
        jnp.where(x % 2 == 0, half, -half),
        jnp.where((x + y) % 2 == 0, half, -half),
        jnp.where((x + y + z) % 2 == 0, half, -half),
    ]
    zero = jnp.zeros((4, LANES), F32)
    sides = ((low, low_x), (own, own_x), (high, high_x))

    def place(k, parts):
        for i in range(2):
            cut = [v[4 * i : 4 * i + 4] for v in parts]
            out[k, i, 0:4] = cut[0]
            out[k, i, 4:8] = cut[1]
            out[k, i, 8:12] = cut[2]
            out[k, i, 12:16] = zero

    for mu in range(4):
        signs = [
            jnp.where(t == 3, etas[mu] * flip[i], etas[mu]) if mu == 3 else etas[mu]
            for i in range(3)
        ]

        def one(k, _, mu=mu, signs=signs):
            j = 18 * (mu % 2) + k
            parts = []
            for (a, b), s in zip(sides, signs):
                mine, theirs = a[j], b[j]
                w = jnp.where(first, mine, theirs) if mu < 2 else jnp.where(first, theirs, mine)
                parts.append(w * s)
            place(18 * mu + k, parts)
            return 0

        lax.fori_loop(0, 18, one, 0)
    for k in range(6):
        place(72 + k, [a[36 + k] for a, _ in sides])

    def pack(k, _):
        for i in range(2):
            up[2 * k + i] = out[2 * k + i, 1, 0:8]
            down[2 * k + i] = out[2 * k + i, 0, 0:8]
            up[102 + k, 4 * i : 4 * i + 4] = out[2 * k + i, 1, 8:12]
            down[84 + k, 4 * i : 4 * i + 4] = out[2 * k + i, 0, 8:12]
        return 0

    lax.fori_loop(0, 36, pack, 0)
    for k in range(9):
        for i in range(2):
            up[72 + 2 * k + i] = out[2 * k + i, 0, 0:8]
            up[138 + k, 4 * i : 4 * i + 4] = out[2 * k + i, 0, 8:12]
    for k in range(6):
        for i in range(2):
            up[90 + 2 * k + i] = out[72 + k, i, 0:8]
            down[72 + 2 * k + i] = out[72 + k, i, 0:8]
            up[147 + k, 4 * i : 4 * i + 4] = out[72 + k, i, 8:12]
            down[120 + k, 4 * i : 4 * i + 4] = out[72 + k, i, 8:12]


UP_N = 153
DOWN_N = 126


def wide_field_kernel(own, low, high, out):
    for k in range(6):
        for x in range(2):
            c = slice(4 * x, 4 * x + 4)
            out[2 * k + x, 0:4] = low[k, c]
            out[2 * k + x, 4:8] = own[k, c]
            out[12 + k, c] = high[k, c]


def put_wide(dst, k, x, msg):
    dst[0:8] = msg[2 * k + x]
    dst[8:12] = msg[12 + k, 4 * x : 4 * x + 4]


def z_ahead(v, vy, z):
    return jnp.where(z == NZ - 1, pltpu.roll(vy, LANES - 1, 1), pltpu.roll(v, LANES - 1, 1))


def z_behind(v, vy, z):
    return jnp.where(z == 0, pltpu.roll(vy, 1, 1), pltpu.roll(v, 1, 1))


def times(acc, link, v):
    for r in range(3):
        for c in range(3):
            re, im = link(3 * r + c), link(9 + 3 * r + c)
            acc[r] = acc[r] + re * v[c] - im * v[3 + c]
            acc[3 + r] = acc[3 + r] + re * v[3 + c] + im * v[c]


def adjoint(link, v):
    acc = [None] * 6
    for r in range(3):
        for c in range(3):
            re, im = link(3 * c + r), link(9 + 3 * c + r)
            acc[r] = plus(acc[r], re * v[c] + im * v[3 + c])
            acc[3 + r] = plus(acc[3 + r], re * v[3 + c] - im * v[c])
    return acc


def hop(src, dst, rows, base, links):
    lx, ly, lz, lt = links
    z = lax.broadcasted_iota(jnp.int32, (ROWS, LANES), 1) % NZ

    def one(i, _):
        s = base + i
        v = [src[k, i + 1] for k in range(6)]
        vy = [pltpu.roll(u, NZ, 1) for u in v]
        back = adjoint(lambda k: lz[k, s], v)
        acc = [-z_behind(u, pltpu.roll(u, NZ, 1), z) for u in back]
        times(acc, lambda k: lz[k, s], [z_ahead(u, w, z) for u, w in zip(v, vy)])
        times(acc, lambda k: ly[k, s], vy)
        back = adjoint(lambda k: lt[k, s], v)
        acc = [a - pltpu.roll(u, 1, 0) for a, u in zip(acc, back)]
        times(acc, lambda k: lt[k, s], [pltpu.roll(u, ROWS - 1, 0) for u in v])
        times(acc, lambda k: lx[k, s + 1], [src[k, i + 2] for k in range(6)])
        back = adjoint(lambda k: lx[k, s], [src[k, i] for k in range(6)])
        for k in range(6):
            dst[k, i] = acc[k] - back[k]
        return 0

    lax.fori_loop(0, rows, one, 0)


def put_local(out, src, x0):
    t = None
    for k in range(6):
        for x in range(2):
            out[k, 4 * x : 4 * x + 4] = src[k, x0 + x, 4:8]
        t = plus(t, out[k] * out[k])
    return jnp.sum(t, axis=0, keepdims=True)


def set_row(moments, j, t):
    row = lax.broadcasted_iota(jnp.int32, (8, LANES), 0)
    return jnp.where(row == j, jnp.broadcast_to(t, (8, LANES)), moments)


def message_row(m):
    s = LANES // 2
    while s >= LANES // (2 * STEP):
        m = m + pltpu.roll(m, s, 1)
        s //= 2
    row = lax.broadcasted_iota(jnp.int32, (8, LANES), 0)
    lane = lax.broadcasted_iota(jnp.int32, (8, LANES), 1)
    m = jnp.where(lane // (LANES // (2 * STEP)) == row, m, 0.0)
    return jnp.sum(m, axis=0, keepdims=True)


def two_hops(j, send, m, v0, v1, v2, links, odd, even, ahead, moments):
    hop(v0, v1, 4, 0, links)
    hop(v1, v2, 2, 1, links)
    t = put_local(odd, v1, 1)
    m = set_row(m, j, t) if j < 2 * STEP else m
    t = put_local(even, v2, 0)
    m = set_row(m, j + 1, t) if j + 1 < 2 * STEP else m
    if ahead is not None:
        for k in range(6):
            for x in range(2):
                ahead[2 * k + x] = v2[k, x, 2:10]
    moments[...] = message_row(m) if send else m


def first_hops_kernel(own, low, high, ahead, odd, even, moments, lx, ly, lz, lt, v0, v1, v2):
    links = (lx, ly, lz, lt)

    def side(msg, i, half):
        def at(k):
            c = 4 * (k % 2)
            return msg[i + k], msg[half + k // 2, slice(c, c + 4)]

        return at

    def store(dst, pieces):
        dst[0:8] = pieces[0]
        dst[8:12] = pieces[1]
        dst[12:16] = jnp.zeros((4, LANES), F32)

    behind, behind2, ahead1 = side(low, 0, 102), side(low, 72, 138), side(high, 0, 84)
    for k in range(18):
        store(lx.at[k, 0], behind2(k))
        store(lx.at[k, 1], behind(k))
        lx[k, 2] = own[k, 0]
        lx[k, 3] = own[k, 1]
        store(lx.at[k, 4], ahead1(k))
        for i, ref in ((36, lz), (54, lt)):
            store(ref.at[k, 0], behind(i + k))
            ref[k, 1] = own[i + k, 0]
            ref[k, 2] = own[i + k, 1]
            store(ref.at[k, 3], ahead1(i + k))
        store(v2.at[0, 0], behind(18 + k))
        store(v2.at[0, 1], ahead1(18 + k))
        c, r = (k % 9) % 3, (k % 9) // 3
        ly[k, 0] = v2[0, 0]
        ly[k, 1] = own[18 + k, 0]
        ly[k, 2] = own[18 + k, 1]
        ly[k, 3] = v2[0, 1]
    for i in range(4):
        for r in range(3):
            for c in range(r + 1):
                k, a = 3 * r + c, 3 * c + r
                u, w = ly[k, i], ly[a, i]
                ur, wr = pltpu.roll(u, NZ, 1), pltpu.roll(w, NZ, 1)
                ly[k, i] = u - wr
                if a != k:
                    ly[a, i] = w - ur
                u, w = ly[9 + k, i], ly[9 + a, i]
                ur, wr = pltpu.roll(u, NZ, 1), pltpu.roll(w, NZ, 1)
                ly[9 + k, i] = u + wr
                if a != k:
                    ly[9 + a, i] = w + ur
    m = jnp.zeros((8, LANES), F32)
    t = None
    for k in range(6):
        for x in range(2):
            c = slice(4 * x, 4 * x + 4)
            v0[k, x, 0:8] = low[90 + 2 * k + x]
            v0[k, x, 8:12] = low[147 + k, c]
            v0[k, 2 + x] = own[72 + k, x]
            v0[k, 4 + x, 0:8] = high[72 + 2 * k + x]
            v0[k, 4 + x, 8:12] = high[120 + k, c]
            v = own[72 + k, x, 4:8]
            t = plus(t, v * v)
    m = set_row(m, 0, jnp.sum(t, axis=0, keepdims=True))
    two_hops(1, False, m, v0, v1, v2, links, odd, even, ahead, moments)


def hops_kernel(j, kind, own, low, high, before, lx, ly, lz, lt, *rest):
    links = (lx, ly, lz, lt)
    outs, (v0, v1, v2) = rest[:-3], rest[-3:]
    for k in range(6):
        for x in range(2):
            for i, ref in ((0, low), (2, own), (4, high)):
                if kind == "wide":
                    put_wide(v0.at[k, i + x], k, x, ref)
                else:
                    v0[k, i + x, 2:10] = ref[2 * k + x]
    m = before[...]
    if kind == "wide":
        ahead, odd, even, moments = outs
        two_hops(j, False, m, v0, v1, v2, links, odd, even, ahead, moments)
    elif kind == "next":
        odd, even, moments = outs
        two_hops(j, j + 1 == 2 * STEP, m, v0, v1, v2, links, odd, even, None, moments)
    else:
        (moments,) = outs
        hop(v0.at[:, 1:5], v2, 2, 1, links)
        t = None
        for k in range(6):
            for x in range(2):
                v = v2[k, x, 4:8]
                t = plus(t, v * v)
        m = set_row(m, j, jnp.sum(t, axis=0, keepdims=True))
        moments[...] = message_row(m)


def start_copies(fields, held, sems):
    copies = [pltpu.make_async_copy(f, held.at[i], sems.at[i]) for i, f in enumerate(fields)]
    for c in copies:
        c.start()
    return copies


def restart_kernel(mass, gathered, shifts, *refs):
    n = 3 * STEP + 1
    fields, (r0, r2, r4, moments, state, held, sems) = refs[:n], refs[n:]
    copies = start_copies(fields, held, sems)
    one = jnp.ones((8, LANES), F32)
    m = jnp.full((8, LANES), mass[0], F32)
    m2 = Pair(m * m, jnp.zeros_like(one))
    powers = summed_moments(gathered[...])
    s = first_state(powers, m2, shifts[...])
    leaves, _ = jax.tree_util.tree_flatten((s, [p.h for p in powers[:STEP]]))
    for i, leaf in enumerate(leaves):
        state[i : i + 1] = leaf[0:1]
    rest, top = s["handover"]
    c = [rest[0], -rest[1], rest[2], -rest[3], top]
    for copy in copies:
        copy.wait()
    row = jnp.zeros((8, LANES), F32)
    for i in range(STEP + 1):
        out = {0: r0, 2: r2, 4: r4}.get(i)
        square = None
        for k in range(6):
            t = None
            for j in range(STEP + 1):
                t = plus(t, c[j] * held[i + 2 * j, k])
            if out is not None:
                out[k] = t
            square = plus(square, t * t)
        row = set_row(row, i, jnp.sum(square, axis=0, keepdims=True))
    moments[...] = row


def finish_kernel(tree, mass, gathered, shifts, residues, state, *refs):
    n = 2 * STEP
    fields, (out, act, held, sems) = refs[:n], refs[n:]
    copies = start_copies(fields, held, sems)
    one = jnp.ones((8, LANES), F32)
    m = jnp.full((8, LANES), mass[0], F32)
    m2 = Pair(m * m, jnp.zeros_like(one))
    leaves = [
        jnp.broadcast_to(state[i : i + 1], (8, LANES)) for i in range(tree.num_leaves)
    ]
    s, powers = jax.tree_util.tree_unflatten(tree, leaves)
    s = run_steps(STEP, summed_moments(gathered[...]), s, m2, one, shifts[...], True)
    weights = residues[...]
    c = [
        jnp.broadcast_to(
            jnp.sum(weights * s["sol"][j], axis=1, keepdims=True), (8, LANES)
        )
        for j in range(2 * STEP)
    ]
    t = None
    for j in range(STEP):
        t = plus(t, c[j] * powers[j])
    act[...] = t
    c = [v if j % 2 == 0 else -v for j, v in enumerate(c)]
    for copy in copies:
        copy.wait()
    for k in range(6):
        t = None
        for j in range(2 * STEP):
            t = plus(t, c[j] * held[j, k])
        out[k] = t


def both_ways(x_up, x_down, axis):
    n = lax.axis_size(axis)
    up = [(i, (i + 1) % n) for i in range(n)]
    return lax.ppermute(x_up, axis, up), lax.ppermute(x_down, axis, [(b, a) for a, b in up])


def across(x, step):
    n = lax.axis_size(ZT)
    pairs = [
        (g * n + i, (1 - g) * n + (i + step) % n) for g in range(2) for i in range(n)
    ]
    return lax.ppermute(x, ("grp",) + ZT, pairs)


def everyone(row):
    row = row + lax.ppermute(row, "xy_1", [(0, 1), (1, 0)])
    n = lax.axis_size(REDUCE)
    rows = lax.all_to_all(jnp.broadcast_to(row[None], (n, 1, LANES)), REDUCE, 0, 0, tiled=True)
    rows = rows.reshape(n, LANES)
    return jnp.pad(rows, ((0, -n % 8), (0, 0)))


def field_scratch():
    return [pltpu.VMEM((6, n, ROWS, LANES), F32) for n in (6, 4, 2)]


def held_scratch(n):
    return [pltpu.VMEM((n, *LOCAL), F32), pltpu.SemaphoreType.DMA((n,))]


def state_shape():
    s = jax.ShapeDtypeStruct((8, LANES), F32)
    moments = [Pair(s, s)] * (2 * STEP)
    out = jax.eval_shape(first_state, moments, Pair(s, s), s)
    return jax.tree_util.tree_flatten((out, [s] * STEP))


def on_device(source, links, shifts, residues, mass):
    grp = lax.axis_index("grp")
    place, n_t = lax.axis_index(ZT), lax.axis_size(ZT)
    edges = [(place - 1) % n_t, place, (place + 1) % n_t]
    where = jnp.stack([grp] + [(e == n_t - 1).astype(jnp.int32) for e in edges])
    lane_shifts = jnp.broadcast_to(
        jnp.pad(shifts, (0, LANES - shifts.shape[0]), constant_values=1.0), (8, LANES)
    )
    lane_residues = jnp.broadcast_to(
        jnp.pad(residues, (0, LANES - residues.shape[0])), (8, LANES)
    )
    mine = links.reshape(36, 8, LANES)
    start = source.reshape(LOCAL)
    both = jnp.concatenate([mine, start])
    low, high = both_ways(both, both, ZT)
    wide, up, down = call(
        wide_links_kernel,
        "wide_links",
        [(78, 2, ROWS, LANES), (UP_N, 8, LANES), (DOWN_N, 8, LANES)],
        (where, both, low, high, across(mine, 0), across(mine, 1), across(mine, -1)),
        1,
    )
    low, high = both_ways(up, down, XY)
    ahead_shape, row8, row1 = (12, 8, LANES), (8, LANES), (1, LANES)
    ahead, f1, f2, m, *w = call(
        first_hops_kernel,
        "first_hops",
        [ahead_shape, LOCAL, LOCAL, row8, (18, 5, ROWS, LANES)] + [(18, 4, ROWS, LANES)] * 3,
        (wide, low, high),
        scratch=field_scratch(),
    )

    def hops(field, m, j, kind):
        low, high = both_ways(field, field, XY)
        outs = {
            "wide": [ahead_shape, LOCAL, LOCAL, row8],
            "next": [LOCAL, LOCAL, row1 if j + 1 == 2 * STEP else row8],
            "last": [row1],
        }[kind]
        body = functools.partial(hops_kernel, j, kind)
        return call(
            body, "hops", outs, (field, low, high, m, *w), scratch=field_scratch()
        )

    def taller(field):
        low, high = both_ways(field, field, ZT)
        return call(wide_field_kernel, "wide_field", [(18, 8, LANES)], (field, low, high))[0]

    f3, f4, m = hops(ahead, m, 3, "next")
    ahead, f5, f6, m = hops(taller(f4), m, 5, "wide")
    f7, f8, row = hops(ahead, m, 7, "next")
    gathered = everyone(row)
    ahead, f9, f10, m = hops(taller(f8), m, 9, "wide")
    f11, f12, _ = hops(ahead, m, 11, "next")
    leaves, tree = state_shape()
    count = -(-len(leaves) // 8) * 8
    chain = (start, f1, f2, f3, f4, f5, f6, f7, f8, f9, f10, f11, f12)
    r0, r2, r4, m, state = call(
        restart_kernel,
        "restart",
        [LOCAL, LOCAL, LOCAL, row8, (count, LANES)],
        (mass, gathered, lane_shifts, *chain),
        1,
        len(chain),
        held_scratch(len(chain)),
    )
    ahead, _, r6, m = hops(taller(r4), m, 5, "wide")
    (row,) = hops(ahead, m, 7, "last")
    basis = (start, f2, f4, f6, r0, r2, r4, r6)
    rational, act = call(
        functools.partial(finish_kernel, tree),
        "finish",
        [LOCAL, row8],
        (mass, everyone(row), lane_shifts, lane_residues, state, *basis),
        1,
        len(basis),
        held_scratch(len(basis)),
    )
    act = act[0:1]
    total = act + lax.ppermute(act, "grp", [(0, 1), (1, 0)])
    sites = source.shape[3] * lax.axis_size(XY) * source.shape[4] * n_t * LANES
    sites *= source.shape[0] * lax.axis_size("grp")
    return (rational.reshape(source.shape), (total / sites)[0, 0:1])


def solution(mesh):
    if mesh.size == 512:
        shape = (mesh.shape["grp"], 4, 4, 8, 2)
    else:
        shape = (mesh.shape["grp"], mesh.shape["zt"], 1, mesh.shape["xy"] // 2, 2)
    torus = Mesh(mesh.devices.reshape(shape), ("grp", "zt_0", "zt_1", "xy_0", "xy_1"))
    placed = (
        P("grp", None, None, XY, ZT, None),
        P("grp", None, None, None, XY, ZT, None),
        P(),
        P(),
        P(),
    )
    return jax.shard_map(
        on_device,
        mesh=torus,
        in_specs=placed,
        out_specs=(P("grp", None, None, XY, ZT, None), P()),
        check_vma=False,
    )
```

time: 218 us -> 190 us (0.87)
  the two profiles are of different devices: /device:TPU:2 before, /device:TPU:8 now
where the time goes in v2:
time: 190 us
  starting transfers between devices  114 us (60%)
  waiting for transfers between devices  50.7 us (27%)
  Pallas kernels  20.2 us (11%)
    ppermute x12, starting transfers between devices, both_ways(): lax.ppermute(x_down, axis, [(b, a) for a, b in up])  48.6 us
    all_to_all x2, starting transfers between devices, everyone(): lax.all_to_all(jnp.broadcast_to(row[None], (n, 1, LANES)), REDUCE, 0, 0,...  27.6 us
    ppermute x12, waiting for transfers between devices, both_ways(): lax.ppermute(x_up, axis, up)  21.3 us
    pallas_call x14, Pallas kernels, call(): pl.pallas_call(body, name=name, in_specs=specs, out_specs=[pl.BlockSpec(m...  20.2 us
    ppermute x3, starting transfers between devices, across(): return lax.ppermute(x, ('grp',) + ZT, pairs)  18.7 us
    all_to_all x2, waiting for transfers between devices, everyone(): lax.all_to_all(jnp.broadcast_to(row[None], (n, 1, LANES)), REDUCE, 0, 0,...  14 us
    ppermute x12, starting transfers between devices, both_ways(): lax.ppermute(x_up, axis, up)  13.5 us
    ppermute x12, waiting for transfers between devices, both_ways(): lax.ppermute(x_down, axis, [(b, a) for a, b in up])  8.13 us
  transfers between devices with their start and end apart: 32, of which 16 were waited for; matrix products, arithmetic and copies ran while one was open for 0% of the time, Pallas kernels for 2%

profile of v2, /device:TPU:8, one launch (start us, length us, event | category | flops | bytes accessed | tf_op | source)
XLA Modules:
  0.0 189.7 jit_solution(14896380706469676732)
XLA Ops:
  1.6 4.5 %collective-permute-start = (f32[42,8,128]{2,1,0:T(8,128)S(1)}, f32[42,8,128]{2,1,0:T(8,128)S(1)}, u32[]{:S(2)}, u32[]{:S(2)}) collective-permute-start(f32[42,8,128]{2,1,0:T(8,128)S(1)} %pad_maximum_fusion.own), channel_id=1, source_target_pairs={{0,16},{16,32},{32,48},{48,64},{64,80},{80,96},{96,112},{112,128},... | collective-permute-start | bytes 516104 | tf_op jit(solution)/shard_map/ppermute | solution.py:633
  6.1 5.6 %collective-permute-start.1 = (f32[42,8,128]{2,1,0:T(8,128)S(1)}, f32[42,8,128]{2,1,0:T(8,128)S(1)}, u32[]{:S(2)}, u32[]{:S(2)}) collective-permute-start(f32[42,8,128]{2,1,0:T(8,128)S(1)} %pad_maximum_fusion.own), channel_id=1, source_target_pairs={{16,0},{32,16},{48,32},{64,48},{80,64},{96,80},{112,96},{128,112},... | collective-permute-start | bytes 516104 | tf_op jit(solution)/shard_map/ppermute | solution.py:633
  11.7 7.7 %collective-permute-start.2 = (f32[36,8,128]{2,1,0:T(8,128)}, f32[36,8,128]{2,1,0:T(8,128)S(1)}, u32[]{:S(2)}, u32[]{:S(2)}) collective-permute-start(f32[36,8,128]{2,1,0:T(8,128)} %bitcast.21), channel_id=1, source_target_pairs={{0,256},{16,272},{32,288},{48,304},{64,320},{80,336},{96,352},{112... | collective-permute-start | bytes 442376 | tf_op jit(solution)/shard_map/ppermute | solution.py:641
  21.3 9.0 %collective-permute-start.4 = (f32[36,8,128]{2,1,0:T(8,128)}, f32[36,8,128]{2,1,0:T(8,128)S(1)}, u32[]{:S(2)}, u32[]{:S(2)}) collective-permute-start(f32[36,8,128]{2,1,0:T(8,128)} %bitcast.23), channel_id=1, source_target_pairs={{0,496},{16,256},{32,272},{48,288},{64,304},{80,320},{96,336},{112... | collective-permute-start | bytes 442376 | tf_op jit(solution)/shard_map/ppermute | solution.py:641
  34.8 4.1 %collective-permute-start.6 = (f32[126,8,128]{2,1,0:T(8,128)S(1)}, f32[126,8,128]{2,1,0:T(8,128)S(1)}, u32[]{:S(2)}, u32[]{:S(2)}) collective-permute-start(f32[126,8,128]{2,1,0:T(8,128)S(1)} %get-tuple-element.41), channel_id=1, source_target_pairs={{1,0},{2,1},{3,2},{4,3},{5,4},{6,5},{7,6},{8,7},{9,8},{10,9},{11,1... | collective-permute-start | bytes 1548296 | tf_op jit(solution)/shard_map/ppermute | solution.py:633
  38.9 6.6 %collective-permute-done.6.high = f32[126,8,128]{2,1,0:T(8,128)S(1)} collective-permute-done((f32[126,8,128]{2,1,0:T(8,128)S(1)}, f32[126,8,128]{2,1,0:T(8,128)S(1)}, u32[]{:S(2)}, u32[]{:S(2)}) %collective-permute-start.6) | collective-permute-done | bytes 516128 | tf_op jit(solution)/shard_map/ppermute | solution.py:633
  46.9 2.0 %first_hops.1 = (f32[12,8,128]{2,1,0:T(8,128)S(1)}, f32[6,8,128]{2,1,0:T(8,128)S(1)}, f32[6,8,128]{2,1,0:T(8,128)S(1)}, f32[8,128]{1,0:T(8,128)S(1)}, f32[18,5,1...) custom-call(f32[78,2,16,128]{3,2,1,0:T(8,128)S(1)} %get-tuple-elemen, ...), custom_call_target="tpu_custom_call" | custom-call | tf_op jit(solution)/shard_map/first_hops/pallas_call | solution.py:280
  48.9 2.9 %collective-permute-start.8 = (f32[12,8,128]{2,1,0:T(8,128)S(1)}, f32[12,8,128]{2,1,0:T(8,128)S(1)}, u32[]{:S(2)}, u32[]{:S(2)}) collective-permute-start(f32[12,8,128]{2,1,0:T(8,128)S(1)} %get-tuple-element.42.own), channel_id=1, source_target_pairs={{1,0},{2,1},{3,2},{4,3},{5,4},{6,5},{7,6},{8,7},{9,8},{10,9},{11,1... | collective-permute-start | bytes 147464 | tf_op jit(solution)/shard_map/ppermute | solution.py:633
  55.2 4.1 %collective-permute-start.10 = (f32[6,8,128]{2,1,0:T(8,128)S(1)}, f32[6,8,128]{2,1,0:T(8,128)S(1)}, u32[]{:S(2)}, u32[]{:S(2)}) collective-permute-start(f32[6,8,128]{2,1,0:T(8,128)S(1)} %get-tuple-element.48.own.refs_4_.refs_2_), channel_id=1, source_target_pairs={{16,0},{32,16},{48,32},{64,48},{80,64},{96,80},{112,96},{128,112},... | collective-permute-start | bytes 73736 | tf_op jit(solution)/shard_map/ppermute | solution.py:633
  59.3 2.7 %collective-permute-start.9 = (f32[6,8,128]{2,1,0:T(8,128)S(1)}, f32[6,8,128]{2,1,0:T(8,128)S(1)}, u32[]{:S(2)}, u32[]{:S(2)}) collective-permute-start(f32[6,8,128]{2,1,0:T(8,128)S(1)} %get-tuple-element.48.own.refs_4_.refs_2_), channel_id=1, source_target_pairs={{0,16},{16,32},{32,48},{48,64},{64,80},{80,96},{96,112},{112,128},... | collective-permute-start | bytes 73736 | tf_op jit(solution)/shard_map/ppermute | solution.py:633
  62.0 7.2 %collective-permute-done.9.low = f32[6,8,128]{2,1,0:T(8,128)S(1)} collective-permute-done((f32[6,8,128]{2,1,0:T(8,128)S(1)}, f32[6,8,128]{2,1,0:T(8,128)S(1)}, u32[]{:S(2)}, u32[]{:S(2)}) %collective-permute-start.9) | collective-permute-done | bytes 24608 | tf_op jit(solution)/shard_map/ppermute | solution.py:633
  69.3 2.9 %collective-permute-start.12 = (f32[18,8,128]{2,1,0:T(8,128)S(1)}, f32[18,8,128]{2,1,0:T(8,128)S(1)}, u32[]{:S(2)}, u32[]{:S(2)}) collective-permute-start(f32[18,8,128]{2,1,0:T(8,128)S(1)} %wide_field.3.own), channel_id=1, source_target_pairs={{1,0},{2,1},{3,2},{4,3},{5,4},{6,5},{7,6},{8,7},{9,8},{10,9},{11,1... | collective-permute-start | bytes 221192 | tf_op jit(solution)/shard_map/ppermute | solution.py:633
  72.2 2.0 %collective-permute-done.11.low = f32[18,8,128]{2,1,0:T(8,128)S(1)} collective-permute-done((f32[18,8,128]{2,1,0:T(8,128)S(1)}, f32[18,8,128]{2,1,0:T(8,128)S(1)}, u32[]{:S(2)}, u32[]{:S(2)}) %collective-permute-start.11) | collective-permute-done | bytes 73760 | tf_op jit(solution)/shard_map/ppermute | solution.py:633
  75.9 3.0 %collective-permute-start.14 = (f32[12,8,128]{2,1,0:T(8,128)S(1)}, f32[12,8,128]{2,1,0:T(8,128)S(1)}, u32[]{:S(2)}, u32[]{:S(2)}) collective-permute-start(f32[12,8,128]{2,1,0:T(8,128)S(1)} %get-tuple-element.50.own), channel_id=1, source_target_pairs={{1,0},{2,1},{3,2},{4,3},{5,4},{6,5},{7,6},{8,7},{9,8},{10,9},{11,1... | collective-permute-start | bytes 147464 | tf_op jit(solution)/shard_map/ppermute | solution.py:633
  86.3 8.1 %collective-permute-start.17 = (f32[6,8,128]{2,1,0:T(8,128)S(1)}, f32[6,8,128]{2,1,0:T(8,128)S(1)}, u32[]{:S(2)}, u32[]{:S(2)}) collective-permute-start(f32[6,8,128]{2,1,0:T(8,128)S(1)} %get-tuple-element.59.own.refs_8_), channel_id=1, source_target_pairs={{16,0},{32,16},{48,32},{64,48},{80,64},{96,80},{112,96},{128,112},... | collective-permute-start | bytes 73736 | tf_op jit(solution)/shard_map/ppermute | solution.py:633
  95.1 12.5 %all-to-all-start = ((f32[128,1,128]{2,1,0:T(1,128)}), f32[128,1,128]{2,1,0:T(1,128)S(1)}, u32[]{:S(2)}, u32[]{:S(2)}) async-start(f32[128,1,128]{2,1,0:T(1,128)} %broadcast_in_dim.23), calls=%async_computation | async-start | bytes 131072 | tf_op jit(solution)/shard_map/all_to_all | solution.py:647
  107.8 2.9 %collective-permute-start.19 = (f32[18,8,128]{2,1,0:T(8,128)S(1)}, f32[18,8,128]{2,1,0:T(8,128)S(1)}, u32[]{:S(2)}, u32[]{:S(2)}) collective-permute-start(f32[18,8,128]{2,1,0:T(8,128)S(1)} %wide_field.4.own), channel_id=1, source_target_pairs={{1,0},{2,1},{3,2},{4,3},{5,4},{6,5},{7,6},{8,7},{9,8},{10,9},{11,1... | collective-permute-start | bytes 221192 | tf_op jit(solution)/shard_map/ppermute | solution.py:633
  110.7 2.3 %collective-permute-done.18.low = f32[18,8,128]{2,1,0:T(8,128)S(1)} collective-permute-done((f32[18,8,128]{2,1,0:T(8,128)S(1)}, f32[18,8,128]{2,1,0:T(8,128)S(1)}, u32[]{:S(2)}, u32[]{:S(2)}) %collective-permute-start.18) | collective-permute-done | bytes 73760 | tf_op jit(solution)/shard_map/ppermute | solution.py:633
  114.9 2.9 %collective-permute-start.21 = (f32[12,8,128]{2,1,0:T(8,128)S(1)}, f32[12,8,128]{2,1,0:T(8,128)S(1)}, u32[]{:S(2)}, u32[]{:S(2)}) collective-permute-start(f32[12,8,128]{2,1,0:T(8,128)S(1)} %get-tuple-element.62.own), channel_id=1, source_target_pairs={{1,0},{2,1},{3,2},{4,3},{5,4},{6,5},{7,6},{8,7},{9,8},{10,9},{11,1... | collective-permute-start | bytes 147464 | tf_op jit(solution)/shard_map/ppermute | solution.py:633
  119.6 2.2 %hops.11 = (f32[6,8,128]{2,1,0:T(8,128)S(1)}, f32[6,8,128]{2,1,0:T(8,128)S(1)}, f32[8,128]{1,0:T(8,128)}) custom-call(f32[12,8,128]{2,1,0:T(8,128)S(1)} %get-tuple-element.62.own, f32[12,8,128]{2,1,0:T(8,128)S(1)} %collective-permute-done.20.low, f32[12,8,128]{2,1,0:T(8,128)S(1)} %collective-permute-done.21.high, f32[8,128]{1,0:T(8,128)S(1)} %get-tuple-element.63.before, ...), custom_call_target="tpu_custom_call" | custom-call | tf_op jit(solution)/shard_map/hops/pallas_call | solution.py:280
  121.8 2.1 %restart.1 = (f32[6,8,128]{2,1,0:T(8,128)S(1)}, f32[6,8,128]{2,1,0:T(8,128)S(1)}, f32[6,8,128]{2,1,0:T(8,128)S(1)}, f32[8,128]{1,0:T(8,128)S(1)}, f32[48,128]{1,0:T(8,128)S(1)}) custom-call(f32[1]{0:T(128)S(6)} %copy.7.mass, f32[128,128]{1,0:T(8,128)S(1)} %bitcast.15, f32[8,128]{1,0:T(8,128)S(1)} %broadcast_in_dim.24.shifts, f32[6,8,128]{2,1,0:T(8,128)S(1)} %bitcast.18, ...), custom_call_target="tpu_custom_call" | custom-call | tf_op jit(solution)/shard_map/restart/pallas_call | solution.py:280
  123.9 3.9 %collective-permute-start.22 = (f32[6,8,128]{2,1,0:T(8,128)S(1)}, f32[6,8,128]{2,1,0:T(8,128)S(1)}, u32[]{:S(2)}, u32[]{:S(2)}) collective-permute-start(f32[6,8,128]{2,1,0:T(8,128)S(1)} %get-tuple-element.66.own.refs_6_), channel_id=1, source_target_pairs={{0,16},{16,32},{32,48},{48,64},{64,80},{80,96},{96,112},{112,128},... | collective-permute-start | bytes 73736 | tf_op jit(solution)/shard_map/ppermute | solution.py:633
  127.9 6.1 %collective-permute-start.23 = (f32[6,8,128]{2,1,0:T(8,128)S(1)}, f32[6,8,128]{2,1,0:T(8,128)S(1)}, u32[]{:S(2)}, u32[]{:S(2)}) collective-permute-start(f32[6,8,128]{2,1,0:T(8,128)S(1)} %get-tuple-element.66.own.refs_6_), channel_id=1, source_target_pairs={{16,0},{32,16},{48,32},{64,48},{80,64},{96,80},{112,96},{128,112},... | collective-permute-start | bytes 73736 | tf_op jit(solution)/shard_map/ppermute | solution.py:633
  135.5 2.9 %collective-permute-start.25 = (f32[18,8,128]{2,1,0:T(8,128)S(1)}, f32[18,8,128]{2,1,0:T(8,128)S(1)}, u32[]{:S(2)}, u32[]{:S(2)}) collective-permute-start(f32[18,8,128]{2,1,0:T(8,128)S(1)} %wide_field.5.own), channel_id=1, source_target_pairs={{1,0},{2,1},{3,2},{4,3},{5,4},{6,5},{7,6},{8,7},{9,8},{10,9},{11,1... | collective-permute-start | bytes 221192 | tf_op jit(solution)/shard_map/ppermute | solution.py:633
  138.5 2.0 %collective-permute-done.24.low = f32[18,8,128]{2,1,0:T(8,128)S(1)} collective-permute-done((f32[18,8,128]{2,1,0:T(8,128)S(1)}, f32[18,8,128]{2,1,0:T(8,128)S(1)}, u32[]{:S(2)}, u32[]{:S(2)}) %collective-permute-start.24) | collective-permute-done | bytes 73760 | tf_op jit(solution)/shard_map/ppermute | solution.py:633
  140.5 2.2 %hops.12 = (f32[12,8,128]{2,1,0:T(8,128)S(1)}, f32[6,8,128]{2,1,0:T(8,128)}, f32[6,8,128]{2,1,0:T(8,128)S(1)}, f32[8,128]{1,0:T(8,128)S(1)}) custom-call(f32[18,8,128]{2,1,0:T(8,128)S(1)} %wide_field.5.own, f32[18,8,128]{2,1,0:T(8,128)S(1)} %collective-permute-done.24.low, f32[18,8,128]{2,1,0:T(8,128)S(1)} %collective-permute-done.25.high, ...), custom_call_target="tpu_custom_call" | custom-call | tf_op jit(solution)/shard_map/hops/pallas_call | solution.py:280
  142.7 3.0 %collective-permute-start.27 = (f32[12,8,128]{2,1,0:T(8,128)S(1)}, f32[12,8,128]{2,1,0:T(8,128)S(1)}, u32[]{:S(2)}, u32[]{:S(2)}) collective-permute-start(f32[12,8,128]{2,1,0:T(8,128)S(1)} %get-tuple-element.68.own), channel_id=1, source_target_pairs={{1,0},{2,1},{3,2},{4,3},{5,4},{6,5},{7,6},{8,7},{9,8},{10,9},{11,1... | collective-permute-start | bytes 147464 | tf_op jit(solution)/shard_map/ppermute | solution.py:633
  152.0 15.0 %all-to-all-start.1 = ((f32[128,1,128]{2,1,0:T(1,128)}), f32[128,1,128]{2,1,0:T(1,128)S(1)}, u32[]{:S(2)}, u32[]{:S(2)}) async-start(f32[128,1,128]{2,1,0:T(1,128)} %broadcast_in_dim.26), calls=%async_computation.1 | async-start | bytes 131072 | tf_op jit(solution)/shard_map/all_to_all | solution.py:647
  167.0 14.0 %all-to-all-done.1 = f32[128,1,128]{2,1,0:T(1,128)S(1)} async-done(((f32[128,1,128]{2,1,0:T(1,128)}), f32[128,1,128]{2,1,0:T(1,128)S(1)}, u32[]{:S(2)}, u32[]{:S(2)}) %all-to-all-start.1) | async-done | bytes 65568 | tf_op jit(solution)/shard_map/all_to_all | solution.py:647
  181.0 2.7 %finish.1 = (f32[6,8,128]{2,1,0:T(8,128)}, f32[8,128]{1,0:T(8,128)S(1)}) custom-call(f32[1]{0:T(128)S(6)} %copy.7.mass, f32[128,128]{1,0:T(8,128)S(1)} %bitcast.16, f32[8,128]{1,0:T(8,128)S(1)} %broadcast_in_dim.24.shifts, f32[8,128]{1,0:T(8,128)S(1)} %broadcast_in_dim.27.residues, f32[48,128]{1,0:T(8,128)S(1)} %get-tuple-element.70.state, ...), custom_call_target="tpu_custom_call" | custom-call | tf_op jit(solution)/shard_map/finish/pallas_call | solution.py:280
  183.7 2.2 %collective-permute-start.29 = (f32[1,128]{1,0:T(1,128)S(1)}, f32[1,128]{1,0:T(1,128)S(1)}, u32[]{:S(2)}, u32[]{:S(2)}) collective-permute-start(f32[1,128]{1,0:T(1,128)S(1)} %slice.6), channel_id=1, source_target_pairs={{0,256},{256,0},{1,257},{257,1},{2,258},{258,2},{3,259},{259,3},{4... | collective-permute-start | bytes 1544 | tf_op jit(solution)/shard_map/ppermute | solution.py:746
  185.9 3.3 %collective-permute-done.29 = f32[1,128]{1,0:T(1,128)S(1)} collective-permute-done((f32[1,128]{1,0:T(1,128)S(1)}, f32[1,128]{1,0:T(1,128)S(1)}, u32[]{:S(2)}, u32[]{:S(2)}) %collective-permute-start.29) | collective-permute-done | bytes 544 | tf_op jit(solution)/shard_map/ppermute | solution.py:746
  (64 shorter events, 33.2 us)
Async XLA Ops:
  1.6 31.7 %collective-permute-start = (f32[42,8,128]{2,1,0:T(8,128)S(1)}, f32[42,8,128]{2,1,0:T(8,128)S(1)}, u32[]{:S(2)}, u32[]{:S(2)}) collective-permute-start(f32[42,8,128]{2,1,0:T(8,128)S(1)} %pad_maximum_fusion.own), channel_id=1, source_target_pairs={{0,16},{16,32},{32,48},{48,64},{64,80},{80,96},{96,112},{112,128},... | collective-permute-start | bytes 516104 | tf_op jit(solution)/shard_map/ppermute | solution.py:633
  6.1 27.2 %collective-permute-start.1 = (f32[42,8,128]{2,1,0:T(8,128)S(1)}, f32[42,8,128]{2,1,0:T(8,128)S(1)}, u32[]{:S(2)}, u32[]{:S(2)}) collective-permute-start(f32[42,8,128]{2,1,0:T(8,128)S(1)} %pad_maximum_fusion.own), channel_id=1, source_target_pairs={{16,0},{32,16},{48,32},{64,48},{80,64},{96,80},{112,96},{128,112},... | collective-permute-start | bytes 516104 | tf_op jit(solution)/shard_map/ppermute | solution.py:633
  11.7 18.8 %collective-permute-start.2 = (f32[36,8,128]{2,1,0:T(8,128)}, f32[36,8,128]{2,1,0:T(8,128)S(1)}, u32[]{:S(2)}, u32[]{:S(2)}) collective-permute-start(f32[36,8,128]{2,1,0:T(8,128)} %bitcast.21), channel_id=1, source_target_pairs={{0,256},{16,272},{32,288},{48,304},{64,320},{80,336},{96,352},{112... | collective-permute-start | bytes 442376 | tf_op jit(solution)/shard_map/ppermute | solution.py:641
  19.4 12.4 %collective-permute-start.3 = (f32[36,8,128]{2,1,0:T(8,128)}, f32[36,8,128]{2,1,0:T(8,128)S(1)}, u32[]{:S(2)}, u32[]{:S(2)}) collective-permute-start(f32[36,8,128]{2,1,0:T(8,128)} %bitcast.22), channel_id=1, source_target_pairs={{0,272},{16,288},{32,304},{48,320},{64,336},{80,352},{96,368},{112... | collective-permute-start | bytes 442376 | tf_op jit(solution)/shard_map/ppermute | solution.py:641
  21.3 12.0 %collective-permute-start.4 = (f32[36,8,128]{2,1,0:T(8,128)}, f32[36,8,128]{2,1,0:T(8,128)S(1)}, u32[]{:S(2)}, u32[]{:S(2)}) collective-permute-start(f32[36,8,128]{2,1,0:T(8,128)} %bitcast.23), channel_id=1, source_target_pairs={{0,496},{16,256},{32,272},{48,288},{64,304},{80,320},{96,336},{112... | collective-permute-start | bytes 442376 | tf_op jit(solution)/shard_map/ppermute | solution.py:641
  34.8 12.1 %collective-permute-start.5 = (f32[153,8,128]{2,1,0:T(8,128)S(1)}, f32[153,8,128]{2,1,0:T(8,128)S(1)}, u32[]{:S(2)}, u32[]{:S(2)}) collective-permute-start(f32[153,8,128]{2,1,0:T(8,128)S(1)} %get-tuple-element.40), channel_id=1, source_target_pairs={{0,1},{1,2},{2,3},{3,4},{4,5},{5,6},{6,7},{7,8},{8,9},{9,10},{10,1... | collective-permute-start | bytes 1880072 | tf_op jit(solution)/shard_map/ppermute | solution.py:633
  34.8 10.7 %collective-permute-start.6 = (f32[126,8,128]{2,1,0:T(8,128)S(1)}, f32[126,8,128]{2,1,0:T(8,128)S(1)}, u32[]{:S(2)}, u32[]{:S(2)}) collective-permute-start(f32[126,8,128]{2,1,0:T(8,128)S(1)} %get-tuple-element.41), channel_id=1, source_target_pairs={{1,0},{2,1},{3,2},{4,3},{5,4},{6,5},{7,6},{8,7},{9,8},{10,9},{11,1... | collective-permute-start | bytes 1548296 | tf_op jit(solution)/shard_map/ppermute | solution.py:633
  48.8 4.7 %collective-permute-start.7 = (f32[12,8,128]{2,1,0:T(8,128)S(1)}, f32[12,8,128]{2,1,0:T(8,128)S(1)}, u32[]{:S(2)}, u32[]{:S(2)}) collective-permute-start(f32[12,8,128]{2,1,0:T(8,128)S(1)} %get-tuple-element.42.own), channel_id=1, source_target_pairs={{0,1},{1,2},{2,3},{3,4},{4,5},{5,6},{6,7},{7,8},{8,9},{9,10},{10,1... | collective-permute-start | bytes 147464 | tf_op jit(solution)/shard_map/ppermute | solution.py:633
  48.9 4.7 %collective-permute-start.8 = (f32[12,8,128]{2,1,0:T(8,128)S(1)}, f32[12,8,128]{2,1,0:T(8,128)S(1)}, u32[]{:S(2)}, u32[]{:S(2)}) collective-permute-start(f32[12,8,128]{2,1,0:T(8,128)S(1)} %get-tuple-element.42.own), channel_id=1, source_target_pairs={{1,0},{2,1},{3,2},{4,3},{5,4},{6,5},{7,6},{8,7},{9,8},{10,9},{11,1... | collective-permute-start | bytes 147464 | tf_op jit(solution)/shard_map/ppermute | solution.py:633
  55.2 6.8 %collective-permute-start.10 = (f32[6,8,128]{2,1,0:T(8,128)S(1)}, f32[6,8,128]{2,1,0:T(8,128)S(1)}, u32[]{:S(2)}, u32[]{:S(2)}) collective-permute-start(f32[6,8,128]{2,1,0:T(8,128)S(1)} %get-tuple-element.48.own.refs_4_.refs_2_), channel_id=1, source_target_pairs={{16,0},{32,16},{48,32},{64,48},{80,64},{96,80},{112,96},{128,112},... | collective-permute-start | bytes 73736 | tf_op jit(solution)/shard_map/ppermute | solution.py:633
  59.3 9.9 %collective-permute-start.9 = (f32[6,8,128]{2,1,0:T(8,128)S(1)}, f32[6,8,128]{2,1,0:T(8,128)S(1)}, u32[]{:S(2)}, u32[]{:S(2)}) collective-permute-start(f32[6,8,128]{2,1,0:T(8,128)S(1)} %get-tuple-element.48.own.refs_4_.refs_2_), channel_id=1, source_target_pairs={{0,16},{16,32},{32,48},{48,64},{64,80},{80,96},{96,112},{112,128},... | collective-permute-start | bytes 73736 | tf_op jit(solution)/shard_map/ppermute | solution.py:633
  69.2 5.0 %collective-permute-start.11 = (f32[18,8,128]{2,1,0:T(8,128)S(1)}, f32[18,8,128]{2,1,0:T(8,128)S(1)}, u32[]{:S(2)}, u32[]{:S(2)}) collective-permute-start(f32[18,8,128]{2,1,0:T(8,128)S(1)} %wide_field.3.own), channel_id=1, source_target_pairs={{0,1},{1,2},{2,3},{3,4},{4,5},{5,6},{6,7},{7,8},{8,9},{9,10},{10,1... | collective-permute-start | bytes 221192 | tf_op jit(solution)/shard_map/ppermute | solution.py:633
  69.3 5.0 %collective-permute-start.12 = (f32[18,8,128]{2,1,0:T(8,128)S(1)}, f32[18,8,128]{2,1,0:T(8,128)S(1)}, u32[]{:S(2)}, u32[]{:S(2)}) collective-permute-start(f32[18,8,128]{2,1,0:T(8,128)S(1)} %wide_field.3.own), channel_id=1, source_target_pairs={{1,0},{2,1},{3,2},{4,3},{5,4},{6,5},{7,6},{8,7},{9,8},{10,9},{11,1... | collective-permute-start | bytes 221192 | tf_op jit(solution)/shard_map/ppermute | solution.py:633
  75.9 4.7 %collective-permute-start.13 = (f32[12,8,128]{2,1,0:T(8,128)S(1)}, f32[12,8,128]{2,1,0:T(8,128)S(1)}, u32[]{:S(2)}, u32[]{:S(2)}) collective-permute-start(f32[12,8,128]{2,1,0:T(8,128)S(1)} %get-tuple-element.50.own), channel_id=1, source_target_pairs={{0,1},{1,2},{2,3},{3,4},{4,5},{5,6},{6,7},{7,8},{8,9},{9,10},{10,1... | collective-permute-start | bytes 147464 | tf_op jit(solution)/shard_map/ppermute | solution.py:633
  75.9 4.7 %collective-permute-start.14 = (f32[12,8,128]{2,1,0:T(8,128)S(1)}, f32[12,8,128]{2,1,0:T(8,128)S(1)}, u32[]{:S(2)}, u32[]{:S(2)}) collective-permute-start(f32[12,8,128]{2,1,0:T(8,128)S(1)} %get-tuple-element.50.own), channel_id=1, source_target_pairs={{1,0},{2,1},{3,2},{4,3},{5,4},{6,5},{7,6},{8,7},{9,8},{10,9},{11,1... | collective-permute-start | bytes 147464 | tf_op jit(solution)/shard_map/ppermute | solution.py:633
  82.5 12.0 %collective-permute-start.15 = (f32[1,128]{1,0:T(1,128)S(1)}, f32[1,128]{1,0:T(1,128)S(1)}, u32[]{:S(2)}, u32[]{:S(2)}) collective-permute-start(f32[1,128]{1,0:T(1,128)S(1)} %get-tuple-element.52), channel_id=1, source_target_pairs={{0,1},{1,0},{2,3},{3,2},{4,5},{5,4},{6,7},{7,6},{8,9},{9,8},{10,11... | collective-permute-start | bytes 1544 | tf_op jit(solution)/shard_map/ppermute | solution.py:645
  84.4 23.3 %collective-permute-start.16 = (f32[6,8,128]{2,1,0:T(8,128)S(1)}, f32[6,8,128]{2,1,0:T(8,128)S(1)}, u32[]{:S(2)}, u32[]{:S(2)}) collective-permute-start(f32[6,8,128]{2,1,0:T(8,128)S(1)} %get-tuple-element.59.own.refs_8_), channel_id=1, source_target_pairs={{0,16},{16,32},{32,48},{48,64},{64,80},{80,96},{96,112},{112,128},... | collective-permute-start | bytes 73736 | tf_op jit(solution)/shard_map/ppermute | solution.py:633
  86.3 21.4 %collective-permute-start.17 = (f32[6,8,128]{2,1,0:T(8,128)S(1)}, f32[6,8,128]{2,1,0:T(8,128)S(1)}, u32[]{:S(2)}, u32[]{:S(2)}) collective-permute-start(f32[6,8,128]{2,1,0:T(8,128)S(1)} %get-tuple-element.59.own.refs_8_), channel_id=1, source_target_pairs={{16,0},{32,16},{48,32},{64,48},{80,64},{96,80},{112,96},{128,112},... | collective-permute-start | bytes 73736 | tf_op jit(solution)/shard_map/ppermute | solution.py:633
  95.1 26.6 %all-to-all-start = ((f32[128,1,128]{2,1,0:T(1,128)}), f32[128,1,128]{2,1,0:T(1,128)S(1)}, u32[]{:S(2)}, u32[]{:S(2)}) async-start(f32[128,1,128]{2,1,0:T(1,128)} %broadcast_in_dim.23), calls=%async_computation | async-start | bytes 131072 | tf_op jit(solution)/shard_map/all_to_all | solution.py:647
  107.7 5.2 %collective-permute-start.18 = (f32[18,8,128]{2,1,0:T(8,128)S(1)}, f32[18,8,128]{2,1,0:T(8,128)S(1)}, u32[]{:S(2)}, u32[]{:S(2)}) collective-permute-start(f32[18,8,128]{2,1,0:T(8,128)S(1)} %wide_field.4.own), channel_id=1, source_target_pairs={{0,1},{1,2},{2,3},{3,4},{4,5},{5,6},{6,7},{7,8},{8,9},{9,10},{10,1... | collective-permute-start | bytes 221192 | tf_op jit(solution)/shard_map/ppermute | solution.py:633
  107.8 5.2 %collective-permute-start.19 = (f32[18,8,128]{2,1,0:T(8,128)S(1)}, f32[18,8,128]{2,1,0:T(8,128)S(1)}, u32[]{:S(2)}, u32[]{:S(2)}) collective-permute-start(f32[18,8,128]{2,1,0:T(8,128)S(1)} %wide_field.4.own), channel_id=1, source_target_pairs={{1,0},{2,1},{3,2},{4,3},{5,4},{6,5},{7,6},{8,7},{9,8},{10,9},{11,1... | collective-permute-start | bytes 221192 | tf_op jit(solution)/shard_map/ppermute | solution.py:633
  114.6 5.0 %collective-permute-start.20 = (f32[12,8,128]{2,1,0:T(8,128)S(1)}, f32[12,8,128]{2,1,0:T(8,128)S(1)}, u32[]{:S(2)}, u32[]{:S(2)}) collective-permute-start(f32[12,8,128]{2,1,0:T(8,128)S(1)} %get-tuple-element.62.own), channel_id=1, source_target_pairs={{0,1},{1,2},{2,3},{3,4},{4,5},{5,6},{6,7},{7,8},{8,9},{9,10},{10,1... | collective-permute-start | bytes 147464 | tf_op jit(solution)/shard_map/ppermute | solution.py:633
  114.9 4.6 %collective-permute-start.21 = (f32[12,8,128]{2,1,0:T(8,128)S(1)}, f32[12,8,128]{2,1,0:T(8,128)S(1)}, u32[]{:S(2)}, u32[]{:S(2)}) collective-permute-start(f32[12,8,128]{2,1,0:T(8,128)S(1)} %get-tuple-element.62.own), channel_id=1, source_target_pairs={{1,0},{2,1},{3,2},{4,3},{5,4},{6,5},{7,6},{8,7},{9,8},{10,9},{11,1... | collective-permute-start | bytes 147464 | tf_op jit(solution)/shard_map/ppermute | solution.py:633
  123.9 10.1 %collective-permute-start.22 = (f32[6,8,128]{2,1,0:T(8,128)S(1)}, f32[6,8,128]{2,1,0:T(8,128)S(1)}, u32[]{:S(2)}, u32[]{:S(2)}) collective-permute-start(f32[6,8,128]{2,1,0:T(8,128)S(1)} %get-tuple-element.66.own.refs_6_), channel_id=1, source_target_pairs={{0,16},{16,32},{32,48},{48,64},{64,80},{80,96},{96,112},{112,128},... | collective-permute-start | bytes 73736 | tf_op jit(solution)/shard_map/ppermute | solution.py:633
  127.9 7.6 %collective-permute-start.23 = (f32[6,8,128]{2,1,0:T(8,128)S(1)}, f32[6,8,128]{2,1,0:T(8,128)S(1)}, u32[]{:S(2)}, u32[]{:S(2)}) collective-permute-start(f32[6,8,128]{2,1,0:T(8,128)S(1)} %get-tuple-element.66.own.refs_6_), channel_id=1, source_target_pairs={{16,0},{32,16},{48,32},{64,48},{80,64},{96,80},{112,96},{128,112},... | collective-permute-start | bytes 73736 | tf_op jit(solution)/shard_map/ppermute | solution.py:633
  135.5 5.0 %collective-permute-start.24 = (f32[18,8,128]{2,1,0:T(8,128)S(1)}, f32[18,8,128]{2,1,0:T(8,128)S(1)}, u32[]{:S(2)}, u32[]{:S(2)}) collective-permute-start(f32[18,8,128]{2,1,0:T(8,128)S(1)} %wide_field.5.own), channel_id=1, source_target_pairs={{0,1},{1,2},{2,3},{3,4},{4,5},{5,6},{6,7},{7,8},{8,9},{9,10},{10,1... | collective-permute-start | bytes 221192 | tf_op jit(solution)/shard_map/ppermute | solution.py:633
  135.5 5.0 %collective-permute-start.25 = (f32[18,8,128]{2,1,0:T(8,128)S(1)}, f32[18,8,128]{2,1,0:T(8,128)S(1)}, u32[]{:S(2)}, u32[]{:S(2)}) collective-permute-start(f32[18,8,128]{2,1,0:T(8,128)S(1)} %wide_field.5.own), channel_id=1, source_target_pairs={{1,0},{2,1},{3,2},{4,3},{5,4},{6,5},{7,6},{8,7},{9,8},{10,9},{11,1... | collective-permute-start | bytes 221192 | tf_op jit(solution)/shard_map/ppermute | solution.py:633
  142.7 4.7 %collective-permute-start.26 = (f32[12,8,128]{2,1,0:T(8,128)S(1)}, f32[12,8,128]{2,1,0:T(8,128)S(1)}, u32[]{:S(2)}, u32[]{:S(2)}) collective-permute-start(f32[12,8,128]{2,1,0:T(8,128)S(1)} %get-tuple-element.68.own), channel_id=1, source_target_pairs={{0,1},{1,2},{2,3},{3,4},{4,5},{5,6},{6,7},{7,8},{8,9},{9,10},{10,1... | collective-permute-start | bytes 147464 | tf_op jit(solution)/shard_map/ppermute | solution.py:633
  142.7 4.7 %collective-permute-start.27 = (f32[12,8,128]{2,1,0:T(8,128)S(1)}, f32[12,8,128]{2,1,0:T(8,128)S(1)}, u32[]{:S(2)}, u32[]{:S(2)}) collective-permute-start(f32[12,8,128]{2,1,0:T(8,128)S(1)} %get-tuple-element.68.own), channel_id=1, source_target_pairs={{1,0},{2,1},{3,2},{4,3},{5,4},{6,5},{7,6},{8,7},{9,8},{10,9},{11,1... | collective-permute-start | bytes 147464 | tf_op jit(solution)/shard_map/ppermute | solution.py:633
  148.3 3.0 %collective-permute-start.28 = (f32[1,128]{1,0:T(1,128)S(1)}, f32[1,128]{1,0:T(1,128)S(1)}, u32[]{:S(2)}, u32[]{:S(2)}) collective-permute-start(f32[1,128]{1,0:T(1,128)S(1)} %hops.13), channel_id=1, source_target_pairs={{0,1},{1,0},{2,3},{3,2},{4,5},{5,4},{6,7},{7,6},{8,9},{9,8},{10,11... | collective-permute-start | bytes 1544 | tf_op jit(solution)/shard_map/ppermute | solution.py:645
  152.0 29.0 %all-to-all-start.1 = ((f32[128,1,128]{2,1,0:T(1,128)}), f32[128,1,128]{2,1,0:T(1,128)S(1)}, u32[]{:S(2)}, u32[]{:S(2)}) async-start(f32[128,1,128]{2,1,0:T(1,128)} %broadcast_in_dim.26), calls=%async_computation.1 | async-start | bytes 131072 | tf_op jit(solution)/shard_map/all_to_all | solution.py:647
  183.7 5.5 %collective-permute-start.29 = (f32[1,128]{1,0:T(1,128)S(1)}, f32[1,128]{1,0:T(1,128)S(1)}, u32[]{:S(2)}, u32[]{:S(2)}) collective-permute-start(f32[1,128]{1,0:T(1,128)S(1)} %slice.6), channel_id=1, source_target_pairs={{0,256},{256,0},{1,257},{257,1},{2,258},{258,2},{3,259},{259,3},{4... | collective-permute-start | bytes 1544 | tf_op jit(solution)/shard_map/ppermute | solution.py:746
  (3 other events, 32.5 us)
